TPU v7x, 32 devices: a 4x4x1 block of a 4x4x8 slice. The times are simulated.
32 devices in a mesh: rep: 1 (over z), dp: 4 (over y), mp: 8 (over x, core).
Axes of the slice: x: 4, y: 4, z: 1, core: 2. Of those that a mesh axis runs over, the one named last changes fastest.
The devices are a block of a 4x4x8 slice.
Arguments:
- x: bfloat16 [4, 2048, 4096], P(('rep', 'dp'), 'mp')
- lengths: int32 [4], P(('rep', 'dp'))
- gamma: bfloat16 [2, 4096], P(None, 'dp')
- wq: bfloat16 [2, 4096, 4096], P(None, 'dp', 'mp')
- wkv: bfloat16 [2, 4096, 512], P(None, 'dp')
- wg: bfloat16 [2, 4096, 16384], P(None, 'dp', 'mp')
- wu: bfloat16 [2, 4096, 16384], P(None, 'dp', 'mp')
- wo: bfloat16 [2, 4096, 4096], P(None, 'mp', 'dp')
- wd: bfloat16 [2, 16384, 4096], P(None, 'mp', 'dp')
Outputs:
- output: bfloat16 [4, 2048, 4096], P(('rep', 'dp'), 'mp')
All inputs are finite; a program needn't handle non-finite values.
Results may differ from a plain program's by a relative error of at most 0.0178136.
Values are sent between devices in bfloat16 or wider.
A program may use at most 768 MiB of HBM per device.

v0:
```python
import math
import jax
import jax.numpy as jnp
from jax import lax
from jax.sharding import PartitionSpec as P

EPS = 1e-6


def norm(x, g):
    xf = x.astype(jnp.float32)
    mu = jnp.mean(xf, axis=-1, keepdims=True)
    xc = xf - mu
    var = jnp.mean(xc * xc, axis=-1, keepdims=True)
    return (xc * lax.rsqrt(var + EPS) * g.astype(jnp.float32)).astype(jnp.bfloat16)


def proj(h, w):
    return jnp.einsum('btd,de->bte', h, w, preferred_element_type=jnp.float32)


def attend(q, k, v, lengths, q0):
    nb, tq, nh, dh = q.shape
    tk = k.shape[1]
    qb = math.gcd(tq, 128)
    nblk = tq // qb
    qs = q.reshape(nb * nblk, qb, nh, dh)
    kpos = jnp.arange(tk)

    def blk(args):
        qi, i = args
        bi = i // nblk
        qpos = q0 + (i % nblk) * qb + jnp.arange(qb)
        s = jnp.einsum('qhd,kd->hqk', qi, k[bi], preferred_element_type=jnp.float32) * (dh ** -0.5)
        ok = (kpos[None, :] <= qpos[:, None]) & (kpos[None, :] < lengths[bi])
        s = jnp.where(ok[None], s, -1e30)
        p = jax.nn.softmax(s, axis=-1).astype(jnp.bfloat16)
        return jnp.einsum('hqk,kd->qhd', p, v[bi], preferred_element_type=jnp.float32).astype(jnp.bfloat16)

    o = lax.map(blk, (qs, jnp.arange(nb * nblk)))
    return o.reshape(nb, tq, nh * dh)


def layer(x, lengths, g, wq, wkv, wg, wu, wo, wd):
    g = lax.all_gather(g, 'dp', axis=0, tiled=True)
    wq = lax.all_gather(wq, 'dp', axis=0, tiled=True)
    wkv = lax.all_gather(wkv, 'dp', axis=0, tiled=True)
    wg = lax.all_gather(wg, 'dp', axis=0, tiled=True)
    wu = lax.all_gather(wu, 'dp', axis=0, tiled=True)
    wo = lax.all_gather(wo, 'dp', axis=1, tiled=True)
    wd = lax.all_gather(wd, 'dp', axis=1, tiled=True)
    dh = wkv.shape[1] // 2
    h = lax.all_gather(norm(x, g), 'mp', axis=1, tiled=True)
    nb, t, _ = h.shape
    q = proj(h, wq).astype(jnp.bfloat16)
    kv = proj(h, wkv).astype(jnp.bfloat16)
    gt = proj(h, wg).astype(jnp.bfloat16)
    up = proj(h, wu).astype(jnp.bfloat16)
    m = (jax.nn.silu(gt.astype(jnp.float32)) * up.astype(jnp.float32)).astype(jnp.bfloat16)
    o = attend(q.reshape(nb, t, -1, dh), kv[:, :, :dh], kv[:, :, dh:], lengths, 0)
    z = (jnp.einsum('bte,ed->btd', o, wo, preferred_element_type=jnp.float32)
         + jnp.einsum('btf,fd->btd', m, wd, preferred_element_type=jnp.float32))
    z = lax.psum_scatter(z.astype(jnp.bfloat16), 'mp', scatter_dimension=1, tiled=True)
    return (x.astype(jnp.float32) + z.astype(jnp.float32)).astype(jnp.bfloat16)


def solution(mesh):
    def body(x, lengths, gamma, wq, wkv, wg, wu, wo, wd):
        for l in range(gamma.shape[0]):
            x = layer(x, lengths, gamma[l], wq[l], wkv[l], wg[l], wu[l], wo[l], wd[l])
        return x
    in_specs = (P(('rep', 'dp'), 'mp', None), P(('rep', 'dp')), P(None, 'dp'),
                P(None, 'dp', 'mp'), P(None, 'dp', None), P(None, 'dp', 'mp'),
                P(None, 'dp', 'mp'), P(None, 'mp', 'dp'), P(None, 'mp', 'dp'))
    return jax.shard_map(body, mesh=mesh, in_specs=in_specs,
                         out_specs=P(('rep', 'dp'), 'mp', None), check_vma=False)
```

profile of v0, /device:TPU:97, one launch (start us, length us, event | category | flops | bytes accessed | tf_op | source)
XLA Modules:
  0.0 1680.1 jit_solution(9073010384056745650)
XLA Ops:
  10.5 11.6 all-gather
  30.4 6.1 fusion.148
  36.7 6.0 fusion.147
  42.9 6.0 fusion.149
  49.2 10.0 all-gather.35.cloned.1.call-done
  59.2 85.3 %all-gather.29.cloned.1.call-done = bf16[1,2048,4096]{2,1,0:T(8,128)(2,1)} async-done(((bf16[1,256,4096]{2,1,0:T(8,128)(2,1)}), bf16[1,2048,4096]{2,1,0:T(8,128)(2,1)}) %all-gather.29.cloned.1.call-update) | async-done | bytes 16777232 | tf_op jit(solution)/shard_map/all_gather | solution.py:53
  144.4 13.6 fusion.129
  159.1 32.4 %all-gather.33.cloned.1.call-done = bf16[1,4096,512]{2,1,0:T(8,128)(2,1)} async-done(((bf16[1,1024,512]{2,1,0:T(8,128)(2,1)}), bf16[1,4096,512]{2,1,0:T(8,128)(2,1)}) %all-gather.33.cloned.1.call-update) | async-done | bytes 4194320 | tf_op jit(solution)/shard_map/all_gather | solution.py:46
  191.5 13.6 fusion.104
  207.3 159.1 %while.28 = (s32[]{:T(128)}, bf16[16,128,2,256]{3,1,2,0:T(8,128)(2,1)S(1)}, s32[16]{0:T(128)S(1)}, s32[1]{0:T(128)}, bf16[16,128,2,256]{3,2,1,0:T(2,128)(2,1)}, ...) while((s32[]{:T(128)}, ...), condition=%wide.region_5.6_spmd.clone.clone, body=%wide.region_2.5_spmd.clone.clone.sunk | while | flops 540610688 | bytes 7347466 | solution.py:40
  211.7 3.5 fusion.169
  221.7 3.5 fusion.169
  231.6 3.5 fusion.169
  241.6 3.5 fusion.169
  251.5 3.5 fusion.169
  261.5 3.5 fusion.169
  271.4 3.5 fusion.169
  281.3 3.5 fusion.169
  291.3 3.5 fusion.169
  301.2 3.5 fusion.169
  311.2 3.5 fusion.169
  321.1 3.5 fusion.169
  331.1 3.5 fusion.169
  341.0 3.5 fusion.169
  360.9 3.5 fusion.169
  369.5 18.1 %fusion.100 = f32[2048,4096]{1,0:T(8,128)} fusion(bf16[1,512,4096]{2,1,0:T(8,128)(2,1)} %all-gather.37.cloned.1.call-done, bf16[64,8,16,128]{3,2,1,0:T(8,128)(2,1)} %bitcast.212), kind=kOutput, calls=%fused_computation.112 | convolution fusion | flops 8589934592 | bytes 39845888 | tf_op jit(solution)/shard_map/bte,ed->btd/dot_general | solution.py:61
  387.6 5.5 all-gather.41.cloned.1.call-done
  393.1 42.5 %fusion.58 = bf16[2048,2048]{1,0:T(8,128)(2,1)} fusion(bf16[1,4096,2048]{2,1,0:T(8,128)(2,1)} %all-gather.41.cloned.1.call-done, bf16[1,2048,4096]{2,1,0:T(8,128)(2,1)} %all-gather.29.cloned.1.call-done), kind=kOutput, calls=%fused_computation.70 | convolution fusion | flops 34359738368 | bytes 41943040 | tf_op jit(solution)/shard_map/btd,de->bte/dot_general | solution.py:19
  435.6 112.2 %all-gather.39.cloned.1.call-done = bf16[1,4096,2048]{2,1,0:T(8,128)(2,1)} async-done(((bf16[1,1024,2048]{2,1,0:T(8,128)(2,1)}), bf16[1,4096,2048]{2,1,0:T(8,128)(2,1)}) %all-gather.39.cloned.1.call-update) | async-done | bytes 16777232 | tf_op jit(solution)/shard_map/all_gather | solution.py:48
  547.8 42.9 %fusion.60 = bf16[2048,2048]{1,0:T(8,128)(2,1)} fusion(bf16[1,4096,2048]{2,1,0:T(8,128)(2,1)} %all-gather.39.cloned.1.call-done, bf16[1,2048,4096]{2,1,0:T(8,128)(2,1)} %all-gather.29.cloned.1.call-done), kind=kOutput, calls=%fused_computation.72 | convolution fusion | flops 34359738368 | bytes 41943040 | tf_op jit(solution)/shard_map/btd,de->bte/dot_general | solution.py:19
  590.7 112.0 %all-gather.43.cloned.1.call-done = bf16[1,2048,4096]{2,1,0:T(8,128)(2,1)} async-done(((bf16[1,2048,1024]{2,1,0:T(8,128)(2,1)}), bf16[1,2048,4096]{2,1,0:T(8,128)(2,1)}) %all-gather.43.cloned.1.call-update) | async-done | bytes 16777232 | tf_op jit(solution)/shard_map/all_gather | solution.py:51
  702.7 47.9 %fusion.70 = bf16[1,2048,4096]{2,1,0:T(8,128)(2,1)} fusion(f32[2048,4096]{1,0:T(8,128)} %fusion.100, bf16[1,2048,4096]{2,1,0:T(8,128)(2,1)} %all-gather.43.cloned.1.call-done, bf16[2048,2048]{1,0:T(8,128)(2,1)} %fusion.58, bf16[2048,2048]{1,0:T(8,128)(2,1)} %fusion.60), kind=kOutput, calls=%fused_computation.82 | convolution fusion | flops 34410070016 | bytes 83886080 | tf_op jit(solution)/shard_map/btf,fd->btd/dot_general | solution.py:62
  751.5 9.2 all-gather.7
  760.8 80.1 %reduce-scatter.3.cloned.1.call-done = bf16[1,256,4096]{2,1,0:T(8,128)(2,1)} async-done(((bf16[1,2048,4096]{2,1,0:T(8,128)(2,1)}), bf16[1,256,4096]{2,1,0:T(8,128)(2,1)}) %reduce-scatter.3.cloned.1.call-update) | async-done | bytes 2097168 | tf_op jit(solution)/shard_map/reduce_scatter | solution.py:63
  850.5 37.4 %all-gather.47.cloned.1.call-done = bf16[1,4096,512]{2,1,0:T(8,128)(2,1)} async-done(((bf16[1,1024,512]{2,1,0:T(8,128)(2,1)}), bf16[1,4096,512]{2,1,0:T(8,128)(2,1)}) %all-gather.47.cloned.1.call-update) | async-done | bytes 4194320 | tf_op jit(solution)/shard_map/all_gather | solution.py:47
  887.9 85.1 %all-gather.31.cloned.1.call-done = bf16[1,2048,4096]{2,1,0:T(8,128)(2,1)} async-done(((bf16[1,256,4096]{2,1,0:T(8,128)(2,1)}), bf16[1,2048,4096]{2,1,0:T(8,128)(2,1)}) %all-gather.31.cloned.1.call-update) | async-done | bytes 16777232 | tf_op jit(solution)/shard_map/all_gather | solution.py:53
  973.0 13.6 fusion.124
  987.7 32.4 %all-gather.45.cloned.1.call-done = bf16[1,4096,512]{2,1,0:T(8,128)(2,1)} async-done(((bf16[1,1024,512]{2,1,0:T(8,128)(2,1)}), bf16[1,4096,512]{2,1,0:T(8,128)(2,1)}) %all-gather.45.cloned.1.call-update) | async-done | bytes 4194320 | tf_op jit(solution)/shard_map/all_gather | solution.py:46
  1020.0 13.6 fusion.114
  1035.9 163.9 %while.29 = (s32[]{:T(128)}, bf16[16,128,2,256]{3,1,2,0:T(8,128)(2,1)S(1)}, s32[16]{0:T(128)S(1)}, s32[1]{0:T(128)}, bf16[16,128,2,256]{3,2,1,0:T(2,128)(2,1)}, ...) while((s32[]{:T(128)}, ...), condition=%wide.region_12.13_spmd.clone.clone, body=%wide.region_9.12_spmd.clone.clone.sunk | while | flops 540610688 | bytes 7347466 | solution.py:40
  1202.9 18.0 %fusion.96 = f32[2048,4096]{1,0:T(8,128)} fusion(bf16[1,512,4096]{2,1,0:T(8,128)(2,1)} %all-gather.49.cloned.1.call-done, bf16[64,8,16,128]{3,2,1,0:T(8,128)(2,1)} %bitcast.213), kind=kOutput, calls=%fused_computation.108 | convolution fusion | flops 8589934592 | bytes 39845888 | tf_op jit(solution)/shard_map/bte,ed->btd/dot_general | solution.py:61
  1221.7 42.5 %fusion.47 = bf16[2048,2048]{1,0:T(8,128)(2,1)} fusion(bf16[1,4096,2048]{2,1,0:T(8,128)(2,1)} %all-gather.53.cloned.1.call-done, bf16[1,2048,4096]{2,1,0:T(8,128)(2,1)} %all-gather.31.cloned.1.call-done), kind=kOutput, calls=%fused_computation.59 | convolution fusion | flops 34359738368 | bytes 41943040 | tf_op jit(solution)/shard_map/btd,de->bte/dot_general | solution.py:19
  1264.2 112.3 %all-gather.51.cloned.1.call-done = bf16[1,4096,2048]{2,1,0:T(8,128)(2,1)} async-done(((bf16[1,1024,2048]{2,1,0:T(8,128)(2,1)}), bf16[1,4096,2048]{2,1,0:T(8,128)(2,1)}) %all-gather.51.cloned.1.call-update) | async-done | bytes 16777232 | tf_op jit(solution)/shard_map/all_gather | solution.py:48
  1376.5 42.7 %fusion.49 = bf16[2048,2048]{1,0:T(8,128)(2,1)} fusion(bf16[1,4096,2048]{2,1,0:T(8,128)(2,1)} %all-gather.51.cloned.1.call-done, bf16[1,2048,4096]{2,1,0:T(8,128)(2,1)} %all-gather.31.cloned.1.call-done), kind=kOutput, calls=%fused_computation.61 | convolution fusion | flops 34359738368 | bytes 41943040 | tf_op jit(solution)/shard_map/btd,de->bte/dot_general | solution.py:19
  1419.2 112.1 %all-gather.55.cloned.1.call-done = bf16[1,2048,4096]{2,1,0:T(8,128)(2,1)} async-done(((bf16[1,2048,1024]{2,1,0:T(8,128)(2,1)}), bf16[1,2048,4096]{2,1,0:T(8,128)(2,1)}) %all-gather.55.cloned.1.call-update) | async-done | bytes 16777232 | tf_op jit(solution)/shard_map/all_gather | solution.py:51
  1531.2 47.9 %fusion.73 = bf16[1,2048,4096]{2,1,0:T(8,128)(2,1)} fusion(f32[2048,4096]{1,0:T(8,128)} %fusion.96, bf16[1,2048,4096]{2,1,0:T(8,128)(2,1)} %all-gather.55.cloned.1.call-done, bf16[2048,2048]{1,0:T(8,128)(2,1)} %fusion.47, bf16[2048,2048]{1,0:T(8,128)(2,1)} %fusion.49), kind=kOutput, calls=%fused_computation.83 | convolution fusion | flops 34410070016 | bytes 83886080 | tf_op jit(solution)/shard_map/btf,fd->btd/dot_general | solution.py:62
  1579.2 90.2 %reduce-scatter.5.cloned.1.call-done = bf16[1,256,4096]{2,1,0:T(8,128)(2,1)} async-done(((bf16[1,2048,4096]{2,1,0:T(8,128)(2,1)}), bf16[1,256,4096]{2,1,0:T(8,128)(2,1)}) %reduce-scatter.5.cloned.1.call-update) | async-done | bytes 2097168 | tf_op jit(solution)/shard_map/reduce_scatter | solution.py:63
  1669.4 3.7 fusion.95
  (284 shorter events, 243.6 us)
Async XLA Ops:
  6.5 3.3 copy-start.5
  6.5 15.5 copy-start.2
  6.6 52.6 %all-gather.35.cloned.1.call-start = ((), (), s32[]{:S(2)}) async-start(), calls=%async_computation.7 | async-start | bytes 5242880 | tf_op jit(solution)/shard_map/all_gather | solution.py:47
  9.8 134.6 %all-gather.29.cloned.1.call-start = ((), (), s32[]{:S(2)}) async-start(), calls=%async_computation.2 | async-start | bytes 18874368 | tf_op jit(solution)/shard_map/all_gather | solution.py:53
  25.4 3.4 copy-start.4
  25.4 166.1 %all-gather.33.cloned.1.call-start = ((), (), s32[]{:S(2)}) async-start(), calls=%async_computation.6 | async-start | bytes 5242880 | tf_op jit(solution)/shard_map/all_gather | solution.py:46
  28.7 340.9 %all-gather.37.cloned.1.call-start = ((), (), s32[]{:S(2)}) async-start(), calls=%async_computation.8 | async-start | bytes 5242880 | tf_op jit(solution)/shard_map/all_gather | solution.py:50
  30.3 362.8 %all-gather.41.cloned.1.call-start = ((), (), s32[]{:S(2)}) async-start(), calls=%async_computation.10 | async-start | bytes 20971520 | tf_op jit(solution)/shard_map/all_gather | solution.py:49
  36.6 511.2 %all-gather.39.cloned.1.call-start = ((), (), s32[]{:S(2)}) async-start(), calls=%async_computation.9 | async-start | bytes 20971520 | tf_op jit(solution)/shard_map/all_gather | solution.py:48
  42.8 659.9 %all-gather.43.cloned.1.call-start = ((), (), s32[]{:S(2)}) async-start(), calls=%async_computation.11 | async-start | bytes 20971520 | tf_op jit(solution)/shard_map/all_gather | solution.py:51
  48.9 792.0 %reduce-scatter.3.cloned.1.call-start = ((), (), s32[]{:S(2)}) async-start(), calls=%async_computation.3 | async-start | bytes 18874368 | tf_op jit(solution)/shard_map/reduce_scatter | solution.py:63
  750.6 0.9 copy-start.6
  750.6 90.2 %copy-start.3 = (bf16[1,256,4096]{2,1,0:T(8,128)(2,1)S(1)}, bf16[1,256,4096]{2,1,0:T(8,128)(2,1)}, u32[]{:S(2)}) copy-start(bf16[1,256,4096]{2,1,0:T(8,128)(2,1)} %param.13) | copy-start | bytes 6291460
  750.7 137.2 %all-gather.47.cloned.1.call-start = ((), (), s32[]{:S(2)}) async-start(), calls=%async_computation.13 | async-start | bytes 5242880 | tf_op jit(solution)/shard_map/all_gather | solution.py:47
  751.5 221.5 %all-gather.31.cloned.1.call-start = ((), (), s32[]{:S(2)}) async-start(), calls=%async_computation.4 | async-start | bytes 18874368 | tf_op jit(solution)/shard_map/all_gather | solution.py:53
  843.3 1.3 copy-start
  846.9 173.2 %all-gather.45.cloned.1.call-start = ((), (), s32[]{:S(2)}) async-start(), calls=%async_computation.12 | async-start | bytes 5242880 | tf_op jit(solution)/shard_map/all_gather | solution.py:46
  847.7 355.2 %all-gather.49.cloned.1.call-start = ((), (), s32[]{:S(2)}) async-start(), calls=%async_computation.14 | async-start | bytes 5242880 | tf_op jit(solution)/shard_map/all_gather | solution.py:50
  848.3 373.4 %all-gather.53.cloned.1.call-start = ((), (), s32[]{:S(2)}) async-start(), calls=%async_computation.16 | async-start | bytes 20971520 | tf_op jit(solution)/shard_map/all_gather | solution.py:49
  849.1 527.4 %all-gather.51.cloned.1.call-start = ((), (), s32[]{:S(2)}) async-start(), calls=%async_computation.15 | async-start | bytes 20971520 | tf_op jit(solution)/shard_map/all_gather | solution.py:48
  849.8 681.5 %all-gather.55.cloned.1.call-start = ((), (), s32[]{:S(2)}) async-start(), calls=%async_computation.17 | async-start | bytes 20971520 | tf_op jit(solution)/shard_map/all_gather | solution.py:51
  850.4 819.0 %reduce-scatter.5.cloned.1.call-start = ((), (), s32[]{:S(2)}) async-start(), calls=%async_computation.5 | async-start | bytes 18874368 | tf_op jit(solution)/shard_map/reduce_scatter | solution.py:63
  1579.2 90.2 %copy-start.1 = (bf16[1,256,4096]{2,1,0:T(8,128)(2,1)S(1)}, bf16[1,256,4096]{2,1,0:T(8,128)(2,1)}, u32[]{:S(2)}) copy-start(bf16[1,256,4096]{2,1,0:T(8,128)(2,1)} %copy-done) | copy-start | bytes 6291460
Sparse Core Ops, SparseCore 0:
  9.9 49.2 all-gather.34
  60.8 83.5 all-gather.28
  146.0 45.4 all-gather.32
  192.9 45.9 all-gather.36
  240.3 152.8 all-gather.40
  394.6 153.1 all-gather.38
  549.4 153.2 all-gather.42
  750.8 90.0 reduce-scatter.2
  842.4 45.4 all-gather.46
  889.3 83.5 all-gather.30
  974.6 45.4 all-gather.44
  1021.5 45.8 all-gather.48
  1069.0 152.7 all-gather.52
  1223.2 153.2 all-gather.50
  1377.9 153.2 all-gather.54
  1579.3 90.0 reduce-scatter.4
where the time goes:
time: 1690 us; the launch traced here: 1680 us
  waiting for transfers between devices  912 us (54%)
  matrix products  534 us (32%)
  local copies, waits for them, and re-layouts  92.7 us (5%)
  loops' own time  64.3 us (4%)
  other arithmetic  41 us (2%)
  blocking collectives  20.8 us (1%)
    dot_general x8, matrix products, proj(): return jnp.einsum('btd,de->bte', h, w, preferred_element_type=jnp.float32)  225 us
    all_gather x2, waiting for transfers between devices, layer(): wg = lax.all_gather(wg, 'dp', axis=0, tiled=True)  224 us
    all_gather x2, waiting for transfers between devices, layer(): wd = lax.all_gather(wd, 'dp', axis=1, tiled=True)  224 us
    all_gather x2, waiting for transfers between devices, layer(): h = lax.all_gather(norm(x, g), 'mp', axis=1, tiled=True)  170 us
    reduce_scatter x2, waiting for transfers between devices, layer(): lax.psum_scatter(z.astype(jnp.bfloat16), 'mp', scatter_dimension=1, tiled...  170 us
    sub x32, matrix products, blk(): p = jax.nn.softmax(s, axis=-1).astype(jnp.bfloat16)  111 us
    dot_general x2, matrix products, layer(): jnp.einsum('btf,fd->btd', m, wd, preferred_element_type=jnp.float32)  95.8 us
    dot_general x32, matrix products, blk(): jnp.einsum('hqk,kd->qhd', p, v[bi], preferred_element_type=jnp.float32)  66.5 us
  transfers between devices with their start and end apart: 16, of which 14 were waited for; matrix products, arithmetic and copies ran while one was open for 34% of the time, Pallas kernels for 0%

commit v1 on v0

v1 whole, which is shorter than its diff:
```python
import functools
import jax
import jax.numpy as jnp
from jax import lax
from jax.experimental import pallas as pl
from jax.experimental.pallas import tpu as pltpu
from jax.sharding import PartitionSpec as P

EPS = 1e-6
BF = jnp.bfloat16
F32 = jnp.float32
MESH = pl.DeviceIdType.MESH
DMA = pltpu.SemaphoreType.DMA
ANY = pl.BlockSpec(memory_space=pl.ANY)
VM = pl.BlockSpec(memory_space=pltpu.VMEM)
NT = 4
CB = 512
RING, LAG = 4, 2
VMEM_LIMIT = 63 * 2**20

OWN, PART, MATE, FAR = SLOTS = range(4)
S, T, F = KINDS = range(3)
GATE, UP = GU = range(2)
MINE, THEIRS = SEQS = range(2)


def scope(name):
    return jax.named_scope(name)


def timed(name):
    def wrap(f):
        @functools.wraps(f)
        def g(*args):
            with scope("_".join([name, *(str(a) for a in args if isinstance(a, int))])):
                return f(*args)
        return g
    return wrap


def dot(a, b):
    return jnp.dot(a, b, preferred_element_type=F32)


def remote(src, dst, s, q, dev):
    return pltpu.make_async_remote_copy(src_ref=src, dst_ref=dst, send_sem=s, recv_sem=q, device_id=dev, device_id_type=MESH)


local = pltpu.make_async_copy


def span(i, n):
    return pl.ds(pl.multiple_of(i * n, n), n)


def each(lo, hi):
    return pl.loop(lo, hi)


class Place:
    def __init__(self, chips):
        self.chips = chips
        self.r = lax.axis_index('dp')
        self.j = lax.axis_index('mp')
        self.chip, self.core = self.j // 2, self.j % 2
        mate = self.r + 1 - 2 * (self.r % 2)
        self.slots = (self.r, 3 - self.r, mate, lax.rem(self.r + 2, 4))
        self.half = self.r // 2
        self.partner, self.mate, self.across = ({'dp': s} for s in self.slots[1:])
        self.sib = {'mp': self.chip * 2 + 1 - self.core}
        self.next, self.prev = self.at(1), self.at(chips - 1)

    def chip_at(self, off):
        return lax.rem(self.chip + off, self.chips)

    def at(self, off):
        return {'mp': self.chip_at(off) * 2 + self.core}

    def meet(self, *peers):
        barrier = pltpu.get_barrier_semaphore()
        for p in peers:
            pl.semaphore_signal(barrier, inc=1, device_id=p, device_id_type=MESH)
        pl.semaphore_wait(barrier, len(peers))


class Pieces:
    def __init__(self, layer, wq, wg, wu, me):
        self.layer, self.me = layer, me
        self.wq, self.w = wq, (wg, wu)
        self.nq = wq.shape[2] // 2
        self.nf = wg.shape[2] // 2
        self.tile = self.nf // NT

    def q(self, half):
        return self.wq.at[self.layer, :, span(half, self.nq)]

    def g(self, half, which, t):
        return self.w[which].at[self.layer, :, span(half * NT + t, self.tile)]

    def tile_part(self, buf, which):
        return buf.at[:, pl.ds(which * self.tile, self.tile)]


def out_rows(layer, half, wo, wd):
    return [w.at[layer, span(half, w.shape[1] // 2), :] for w in (wo, wd)]


def split_rows(o, n):
    return [o.at[pl.ds(0, n), :], o.at[pl.ds(n, o.shape[0] - n), :]]


def front_kernel(layer, chips, *refs):
    first = layer == 0
    it = iter(refs)
    take = lambda n: [next(it) for _ in range(n)]
    x, gam, lens, wq, wkv, wg, wu, wo, wd = take(9)
    if first:
        om, hbuf, s_o, t_o, wkvb, gb, lenb = take(7)
    else:
        wkvb, sq, sg, tq, tg, fq, fg = take(7)
        om, hbuf, s_o, t_o = take(4)
        gb, lenb = gam, lens
    (wqkv, wgu, hv, qkv, hown, hpar, wkvp, sc, ms, os, y_s, y_r, ld, o_s, o_r, kv_sem, hv_sem, ms_sem, os_sem, ag_s, ag_r, own_sem,
     ex_s, ex_r) = it
    me = Place(chips)
    pc = Pieces(layer, wq, wg, wu, me)
    mp = 2 * chips
    tok, d4, nq = x.shape[0], wq.shape[1], pc.nq
    dh = nq

    def at_slot(s, which, t):
        if which < GATE:
            return wqkv.at[s, :, pl.ds(0, nq)]
        return pc.tile_part(wgu.at[s, t], which)

    def raw(half, which, t):
        return pc.q(half) if which < GATE else pc.g(half, which, t)

    def given(q, g, which, t):
        return q if which < GATE else pc.tile_part(g.at[t], which)

    def sem(which, t):
        return 0 if which < GATE else 1 + 2 * t + which

    def load(s, which, t):
        n = sem(which, t)
        if s == OWN:
            src = raw(me.half, which, t)
        else:
            src = given(*{MATE: (sq, sg), PART: (tq, tg), FAR: (fq, fg)}[s] if not first else (), which, t)
        return local(src, at_slot(s, which, t), ld.at[s, n])

    def move(kind, which, t):
        n = sem(which, t)
        if kind == S:
            return remote(raw(me.half, which, t), at_slot(MATE, which, t), y_s.at[S, n], y_r.at[S, n], me.mate)
        if kind == T:
            return remote(raw(1 - me.half, which, t), at_slot(PART, which, t), y_s.at[T, n], y_r.at[T, n], me.partner)
        src = at_slot(PART, which, t) if first else given(tq, tg, which, t)
        return remote(src, at_slot(FAR, which, t), y_s.at[F, n], y_r.at[F, n], me.mate)

    def parts(t):
        return [(GATE - 1, 0)] if t is None else [(w, t) for w in GU]

    def send(kind, *ts):
        for t in ts:
            for p in parts(t):
                move(kind, *p).start()

    @timed('relay')
    def relay(*ts):
        for t in ts:
            for p in parts(t):
                if first:
                    move(T, *p).wait_recv()
                move(F, *p).start()

    def sent_ahead(t):
        return not first and (t is None or (isinstance(t, int) and t < AHEAD))

    @timed('have')
    def have(*ts):
        for t in ts:
            for p in parts(t):
                load(OWN, *p).wait()
                if sent_ahead(t):
                    load(MATE, *p).wait()
                    load(FAR, *p).wait()
                else:
                    move(S, *p).wait_recv()
                    move(F, *p).wait_recv()
                if not first:
                    load(PART, *p).wait()

    every = [None, *range(NT)]
    for t in every:
        for p in parts(t):
            load(OWN, *p).start()
            if not first:
                load(PART, *p).start()
            if sent_ahead(t):
                load(MATE, *p).start()
                load(FAR, *p).start()

    with scope('meet'):
        me.meet(me.sib, me.next, me.prev, me.mate, me.partner, *([me.across] if first else []))

    own_o, oth_o = out_rows(layer, me.half, wo, wd), out_rows(layer, 1 - me.half, wo, wd)
    no = wo.shape[1] // 2
    ahead_o = zip(oth_o + [own_o[0], own_o[1].at[pl.ds(0, s_o.shape[0] - no), :]], split_rows(t_o, no) + split_rows(s_o, no),
                  [me.partner, me.partner, me.mate, me.mate])
    out_moves = [remote(src, dst, o_s.at[n], o_r.at[n], dev) for n, (src, dst, dev) in enumerate(ahead_o)]

    small = []
    if first:
        kv_own = local(wkv.at[:, span(me.j, wkv.shape[1] // mp), :], wkvp.at[:, OWN], own_sem.at[4])
        kv_own.start()
        for s, dev in ((PART, me.partner), (MATE, me.mate), (FAR, me.across)):
            small.append(remote(gam, gb.at[s], ex_s.at[s], ex_r.at[s], dev))
        small.append(remote(lens, lenb.at[THEIRS], ex_s.at[OWN], ex_r.at[OWN], me.partner))
        for c in small:
            c.start()
        gb[OWN] = gam[:, :]
        lenb[MINE] = lens[:, :]
        kv_own.wait()

        def kv_move(kind):
            src, dst, dev = ((OWN, MATE, me.mate), (OWN, PART, me.partner), (PART, FAR, me.mate))[kind]
            return remote(wkvp.at[:, src], wkvp.at[:, dst], ex_s.at[4 + kind], ex_r.at[4 + kind], dev)
        for k in (T, S):
            kv_move(k).start()
            send(k, None)
        send(T, 0)
        with scope('small'):
            for c in small:
                c.wait_recv()
    else:
        for t in range(1, NT):
            send(S, t)
            relay(t)

    @timed('norm')
    def norm():
        rb = 32

        @each(0, tok // rb)
        def _(i):
            rows = span(i, rb)
            xf = x[rows, :].astype(F32)
            mu = jnp.mean(xf, axis=-1, keepdims=True)
            xc = xf - mu
            rstd = lax.rsqrt(jnp.mean(xc * xc, axis=-1, keepdims=True) + EPS)
            for s in SLOTS:
                cols = span(me.slots[s], d4)
                hown[rows, cols] = ((x[rows, cols].astype(F32) - mu) * rstd * gb[s, layer:layer + 1, :]).astype(BF)
    norm()

    SIB, TO, SHARE, PASS, LAST = range(5)

    def gather(g, src, block, part):
        offs = (chips - 1, 1)
        dirs = (me.next, me.prev)

        def idx(off):
            return me.chip_at(off) * 2 + me.core

        def c(kind, k, h):
            n = 4 * kind + 2 * k + h
            sems = (ag_s.at[g, n], ag_r.at[g, n])
            if kind == SIB:
                return remote(src, block(me.j), *sems, me.sib)
            if kind == TO:
                return remote(part(src, h), part(block(me.j), h), *sems, dirs[k])
            b = part(block(idx(2 if kind == LAST else offs[k])), h)
            return remote(b, b, *sems, dirs[k] if kind == PASS else me.sib)

        mine = local(src, block(me.j), own_sem.at[g])
        tag = 'abvw'[g]

        class G:
            @timed('own' + tag)
            def own():
                for h in range(2):
                    for k in range(2):
                        c(TO, k, k ^ h).start()
                c(SIB, 0, 0).start()
                mine.start()

            @timed('near' + tag)
            def near():
                for h in range(2):
                    for k in range(2):
                        c(TO, k, k ^ h).wait_recv()
                        if h == 0:
                            c(PASS, k, k).start()
                        c(SHARE, k, k ^ h).start()

            @timed('far' + tag)
            def far():
                for k in range(2):
                    c(PASS, k, k).wait_recv()
                    c(LAST, k, k).start()

            @timed('has' + tag)
            def has(kind):
                if kind == SIB:
                    mine.wait()
                    c(SIB, 0, 0).wait_recv()
                for k in range(2):
                    if kind == LAST:
                        c(kind, k, k).wait_recv()
                    if kind == SHARE:
                        for h in range(2):
                            c(kind, k, k ^ h).wait_recv()

            def end():
                c(SIB, 0, 0).wait_send()
                for k in range(2):
                    for h in range(2):
                        c(TO, k, h).wait_send()
                        c(SHARE, k, h).wait_send()
                    c(PASS, k, k).wait_send()
                    c(LAST, k, k).wait_send()
        return G

    def h_block(b):
        return lambda j: hbuf.at[b, span(j, tok), :]

    def h_part(ref, k):
        return ref.at[pl.ds(k * (tok // 2), tok // 2), :]

    ga, gb2 = gather(0, hown, h_block(MINE), h_part), gather(1, hpar, h_block(THEIRS), h_part)
    ht = remote(hown, hpar, ex_s.at[7], ex_r.at[7], me.partner)

    rows2 = 2 * tok

    def chip_rows(i):
        return span(me.chip_at(i + i // 2 - 2 * (i // 3)), rows2)

    def hload(i):
        return local(hbuf.at[i // 4, chip_rows(lax.rem(i, 4)), :], hv.at[lax.rem(i, 2)], hv_sem.at[lax.rem(i, 2)])

    def hdot(buf, w):
        acc = None
        for s in SLOTS:
            p = dot(hv[buf, :, span(me.slots[s], d4)], w(s))
            acc = p if acc is None else acc + p
        return acc

    def mcopy(i, t, k):
        w = pc.tile
        return local(ms.at[k], om.at[i // 4, chip_rows(lax.rem(i, 4)), pl.ds(pl.multiple_of(nq + t * w, w), w)], ms_sem.at[k])

    def tile(i, t, m):
        k = lax.rem(m, 2)
        a = hdot(lax.rem(i, 2), lambda s: wgu[s, t])

        @pl.when(m >= 2)
        def _():
            mcopy(i, t, k).wait()
        gt = a[:, :pc.tile].astype(BF).astype(F32)
        up = a[:, pc.tile:].astype(BF).astype(F32)
        ms[k] = (gt * jax.nn.sigmoid(gt) * up).astype(BF)
        mcopy(i, t, k).start()

    def drain():
        for k in range(2):
            mcopy(0, 0, k).wait()

    def any_of(i, marks):
        return functools.reduce(lambda a, b: a | b, [i == g for g in marks])

    def sweep(b, nt, gates, hooks):
        lo = b * chips
        marks = [n for n in gates]

        @each(lo, lo + chips)
        def _(i):
            for g, f in gates.items():
                pl.when(i == g)(f)

            @pl.when(any_of(i, [lo, *marks]))
            def _():
                hload(i).start()

            @pl.when(jnp.logical_not(any_of(i + 1, [lo + chips, *marks])))
            def _():
                hload(i + 1).start()
            hload(i).wait()
            qkv[b, chip_rows(i - lo), :] = hdot(lax.rem(i, 2), lambda s: wqkv[s]).astype(BF)

            @each(0, nt)
            def _(t):
                for n, f in hooks.items():
                    pl.when((i == lo) & (b == MINE) & (t == n))(f)
                tile(i, t, (i - lo) * nt + t)
        drain()

    def late(lo_t, hi_t, lo, hi):
        n = hi - lo
        hload(lo).start()

        @each(0, n * (hi_t - lo_t))
        def _(u):
            i, t = lo + lax.rem(u, n), lo_t + u // n

            @pl.when(lax.rem(u, n) == 0)
            def _():
                have(t)

            @pl.when(u + 1 < n * (hi_t - lo_t))
            def _():
                hload(lo + lax.rem(u + 1, n)).start()
            hload(i).wait()
            tile(i, t, u)
        drain()

    bq, bk = sc.shape[1:]

    @timed('attend')
    def attend(b):
        nblk = qkv.shape[1] // bq
        ratio = bk // bq

        def ocp(i, k):
            return local(os.at[k], om.at[b, span(i, bq), pl.ds(0, dh)], os_sem.at[k])

        def lanes(a, op):
            w = a.shape[1] // ratio // 2
            return functools.reduce(op, [a[:, n * w:(n + 1) * w] for n in range(2 * ratio)])

        @each(0, nblk)
        def _(i):
            q = qkv[b, span(i, bq), pl.ds(0, dh)]
            length = lenb[b, :, :][:1, :1]
            colf = lax.broadcasted_iota(jnp.int32, (1, bk), 1).astype(F32)

            def raw_score(j):
                k = qkv[b, span(j, bk), pl.ds(dh, dh)]
                s = lax.dot_general(q, k, (((1,), (1,)), ((), ())), preferred_element_type=F32) * (dh ** -0.5)
                pos = jnp.broadcast_to(colf + (j * bk).astype(F32), (bq, bk))
                return jnp.where(pos < length, s, -1e30)

            def score(j, m):
                s = raw_score(j)
                sc[j] = s
                return jnp.maximum(m, lanes(s, jnp.maximum))

            last = i // ratio
            row = lax.broadcasted_iota(jnp.int32, (bq, bk), 0) + (i - last * ratio) * bq
            col = lax.broadcasted_iota(jnp.int32, (bq, bk), 1)
            s = jnp.where(col <= row, raw_score(last), -1e30)
            sc[last] = s
            m = jnp.max(lax.fori_loop(0, last, score, lanes(s, jnp.maximum)), axis=1, keepdims=True)

            def expo(j, l):
                p = jnp.exp(sc[j] - m)
                sc[j] = p
                return l + lanes(p, jnp.add)

            l = jnp.sum(lax.fori_loop(0, last + 1, expo, jnp.zeros((bq, bk // ratio // 2), F32)), axis=1, keepdims=True)
            inv = 1.0 / l

            def value(j, o):
                return o + dot((sc[j] * inv).astype(BF), qkv[b, span(j, bk), pl.ds(2 * dh, dh)])

            o = lax.fori_loop(0, last + 1, value, jnp.zeros((bq, dh), F32))
            k = lax.rem(i, 2)

            @pl.when(i >= 2)
            def _():
                ocp(i, k).wait()
            os[k] = o.astype(BF)
            ocp(i, k).start()
        for k in range(2):
            ocp(k, k).wait()

    def kv_load(u):
        s, j = u // mp, lax.rem(u, mp)
        return local(wkvb.at[layer, j, s], wqkv.at[s, span(j, wkvp.shape[2]), pl.ds(nq, 2 * dh)], kv_sem.at[u])

    def kv_loads(go):
        @each(0, 4 * mp)
        def _(u):
            go(kv_load(u))

    def near_of(g):
        def f():
            g.near()
            g.has(SHARE)
        return f

    def far_of(g):
        def f():
            g.far()
            g.has(LAST)
        return f

    def both(*fs):
        def f():
            for g in fs:
                g()
        return f

    def start_b():
        with scope('ht'):
            ht.wait_recv()
        gb2.own()

    ga.own()
    ht.start()
    if first:
        with scope('kvmove'):
            kv_move(T).wait_recv()
            kv_move(F).start()
            kv_move(S).wait_recv()
        send(S, 0)
        send(T, 1)
        relay(None)
        send(S, 1)
        with scope('kvmove2'):
            kv_move(F).wait_recv()
        gw = [gather(2 + n, wkvp.at[n], lambda j, n=n: wkvb.at[n, j], lambda ref, k: ref.at[pl.ds(2 * k, 2)]) for n in range(2)]
        relay(0)
        send(S, 2)
        send(T, 2)
        send(T, 3)
        ga.near()
        gw[0].own()
        for c in out_moves[:2]:
            c.start()
        ga.far()
        gw[0].near()
        start_b()
        gw[0].far()
        gw[1].own()
        for kind in (SIB, SHARE, LAST):
            gw[0].has(kind)
        kv_loads(lambda c: c.start())
        for kind in (SIB, SHARE, LAST):
            ga.has(kind)
        kv_loads(lambda c: c.wait())
        have(None, 0)

        @each(0, 2)
        def _(b):
            with scope('sweep'):
                sweep(b, 1, {chips: both(lambda: gb2.has(SIB), gb2.near), chips + 1: both(lambda: gb2.has(SHARE), gw[1].near),
                             chips + 3: both(far_of(gb2), gw[1].far)}, {})

            @pl.when(b == MINE)
            def _():
                relay(1)
                send(S, 3)
            attend(b)

            @pl.when(b == MINE)
            def _():
                relay(2)

            @pl.when(b == THEIRS)
            def _():
                relay(3)
                for c in out_moves[2:]:
                    c.start()
        with scope('late'):
            late(1, NT, 0, 2 * chips)
        for kind in (SIB, SHARE, LAST):
            gw[1].has(kind)
    else:
        for c in out_moves:
            c.start()
        kv_loads(lambda c: c.start())
        kv_loads(lambda c: c.wait())
        have(None, 0)

        @each(0, 2)
        def _(b):
            with scope('sweep'):
                sweep(b, 2 + b, {0: lambda: ga.has(SIB), 1: both(near_of(ga), start_b), 3: far_of(ga),
                                 chips: both(lambda: gb2.has(SIB), gb2.near), chips + 1: lambda: gb2.has(SHARE), chips + 3: far_of(gb2)},
                      {1: lambda: have(1)})
            attend(b)

            @pl.when(b == MINE)
            def _():
                with scope('late2'):
                    late(2, 3, 0, chips)
        with scope('late'):
            late(3, NT, 0, 2 * chips)

    with scope('end'):
        for t in every:
            for p in parts(t):
                if not sent_ahead(t):
                    move(S, *p).wait_send()
                    move(F, *p).wait_send()
                if first:
                    move(T, *p).wait_send()
        for c in out_moves:
            c.wait()
        ht.wait_send()
        ga.end()
        gb2.end()
        for c in small:
            c.wait_send()
        if first:
            gw[0].end()
            gw[1].end()
            for k in KINDS:
                kv_move(k).wait_send()


AHEAD = 1


def front(layer, mesh, x, gam, lens, weights, given):
    wq, wkv, wg, wu, wo, wd = weights
    tok, d = x.shape
    mp = mesh.shape['mp']
    chips = mp // 2
    first = layer == 0
    d4 = wq.shape[1]
    nq, nkv, nf = wq.shape[2] // 2, wkv.shape[2], wg.shape[2] // 2
    no, nd = wo.shape[1] // 2, wd.shape[1] // 2
    t = tok * mp
    kvr = wkv.shape[1] // mp
    sds = jax.ShapeDtypeStruct
    outs = [sds((2, t, nq + nf), BF), sds((2, t, d), BF), sds((no + nd // 2, d4), BF), sds((no + nd, d4), BF)]
    specs = [ANY] * 4
    if first:
        outs += [sds((2, mp, 4, kvr, nkv), BF), sds((4, *gam.shape), F32), sds((2, *lens.shape), F32)]
        specs += [ANY, VM, VM]
    npiece = 1 + 2 * NT
    return pl.pallas_call(
        functools.partial(front_kernel, layer, chips), out_shape=outs,
        in_specs=[VM, VM, VM] + [ANY] * (6 + len(given)), out_specs=specs,
        scratch_shapes=[
            pltpu.VMEM((4, d4, nq + nkv), BF), pltpu.VMEM((4, NT, d4, 2 * nf // NT), BF), pltpu.VMEM((2, 2 * tok, d), BF),
            pltpu.VMEM((2, t, nq + nkv), BF), pltpu.VMEM((tok, d), BF), pltpu.VMEM((tok, d), BF),
            pltpu.VMEM((2, 4, kvr, nkv), BF), pltpu.VMEM((t // nq // 2, nq, 2 * nq), F32),
            pltpu.VMEM((2, 2 * tok, nf // NT), BF), pltpu.VMEM((2, nq, nq), BF),
            DMA((3, npiece)), DMA((3, npiece)), DMA((4, npiece)), DMA((4,)), DMA((4,)), DMA((4 * mp,)), DMA((2,)), DMA((2,)), DMA((2,)),
            DMA((4, 20)), DMA((4, 20)), DMA((5,)), DMA((8,)), DMA((8,))],
        compiler_params=pltpu.CompilerParams(vmem_limit_bytes=VMEM_LIMIT, collective_id=2 * layer, has_side_effects=True),
        cost_estimate=pl.CostEstimate(flops=4 * t * d * (nq + nkv + 2 * nf), bytes_accessed=12 * t * d, transcendentals=0),
        name=f"front{layer}")(x, gam, lens, *weights, *given)


def back_kernel(layer, chips, nxt, *refs):
    it = iter(refs)
    take = lambda n: [next(it) for _ in range(n)]
    x, om_h, s_o, t_o, wo, wd = take(6)
    if nxt:
        wq, wg, wu = take(3)
    y = next(it)
    if nxt:
        sq, sg, tq, tg, fq, fg = take(6)
    (om, w, sl, rel, fin, zt, sib, acc, in_sem, w_s, w_r, p_s, p_r, sib_s, sib_r, rel_s, rel_r, fin_s, fin_r, t_s, t_r) = it
    me = Place(chips)
    nb, rows = zt.shape[:2]
    per = w.shape[2] // CB
    no, ns = wo.shape[1] // 2, s_o.shape[0]

    own_o = out_rows(layer, me.half, wo, wd)
    own_rows, mate_rows = split_rows(w.at[OWN], no), split_rows(w.at[MATE], ns)
    loads = [local(om_h.at[THEIRS], om.at[THEIRS], in_sem.at[0]), local(own_o[0], own_rows[0], in_sem.at[1]),
             local(own_o[1], own_rows[1], in_sem.at[2]), local(t_o, w.at[PART], in_sem.at[3]), local(om_h.at[MINE], om.at[MINE], in_sem.at[4]),
             local(s_o, mate_rows[0], in_sem.at[5])]
    for c in loads:
        c.start()
    me.meet(me.sib, me.next, me.prev, me.mate, me.partner)
    to_mate = [remote(own_o[1].at[pl.ds(ns - no, no + own_o[1].shape[0] - ns), :], mate_rows[1], w_s.at[0], w_r.at[0], me.mate), remote(t_o, w.at[FAR], w_s.at[1], w_r.at[1], me.mate)]
    for c in to_mate:
        c.start()
    passing = []
    if nxt:
        pc = Pieces(layer + 1, wq, wg, wu, me)

        def buffers(q, g, nt):
            return [q] + [pc.tile_part(g.at[t], which) for t in range(nt) for which in GU]

        def args(half, nt):
            return [pc.q(half)] + [pc.g(half, which, t) for t in range(nt) for which in GU]

        def ahead(kind, srcs, dsts, dev):
            return [remote(*sd, p_s.at[kind, n], p_r.at[kind, n], dev) for n, sd in enumerate(zip(srcs, dsts))]
        to_s = ahead(S, args(me.half, AHEAD), buffers(sq, sg, AHEAD), me.mate)
        to_t = ahead(T, args(1 - me.half, NT), buffers(tq, tg, NT), me.partner)
        on = ahead(F, buffers(tq, tg, AHEAD), buffers(fq, fg, AHEAD), me.mate)
        for c in to_t + to_s:
            c.start()
        passing = to_s + on + to_t[len(on):]
    with scope('loads'):
        for c in loads[:4]:
            c.wait()

    AWAY, NEAR, JOIN, HOME = range(4)

    def sib_copy(st, b, cb, m):
        k = lax.rem(m, RING)
        return remote(sib.at[k], sl.at[st, b, cb], sib_s.at[k], sib_r.at[st, b, cb], me.sib)

    def away_copy(b, cb):
        return remote(sl.at[AWAY, b, cb], rel.at[b, cb], rel_s.at[b, cb], rel_r.at[b, cb], me.at(1 + 2 * lax.rem(cb, 2)))

    def near_copy(st, b, cb):
        p = lax.rem(st + cb, 2)
        return remote(sl.at[st, b, cb], fin.at[p, b, cb], fin_s.at[p, b, cb], fin_r.at[p, b, cb], me.at(1 + 2 * p))

    def compute(off, st, b, cb, m):
        a = acc.at[lax.rem(m, LAG + 1)]
        a[:, :] = dot(om[b, span(me.chip_at(off), 2 * rows), :], w[cb // per, :, span(lax.rem(cb, per), CB)])

        @pl.when(m >= RING)
        def _():
            sib_copy(st, b, cb, m).wait_send()
        sib[lax.rem(m, RING)] = a[span(1 - me.core, rows), :].astype(BF)
        sib_copy(st, b, cb, m).start()

    def combined(st, b, cb, m):
        sib_copy(st, b, cb, m).wait_recv()
        a = acc.at[lax.rem(m, LAG + 1)]
        return a[span(me.core, rows), :] + sl[st, b, cb].astype(F32)

    def run(n, unit, off, finish):
        @each(0, n + LAG)
        def _(m):
            @pl.when(m < n)
            def _():
                st, b, cb = unit(m)
                compute(off(st, cb), st, b, cb, m)

            @pl.when(m >= LAG)
            def _():
                st, b, cb = unit(m - LAG)
                finish(st, b, cb, combined(st, b, cb, m - LAG))

        for m in range(RING):
            sib_copy(HOME, MINE, 0, m).wait_send()

    @timed('stages')
    def stages(lo, n):
        def away(m):
            return AWAY, 1 - m // n, lo + lax.rem(m, n)

        def away_on(st, b, cb, v):
            sl[st, b, cb] = v.astype(BF)
            away_copy(b, cb).start()
        run(2 * n, away, lambda st, cb: 2, away_on)

        def near(m):
            return NEAR + lax.rem(m // n, 2), 1 - m // (2 * n), lo + lax.rem(m, n)

        def near_on(st, b, cb, v):
            @pl.when(st == NEAR)
            def _():
                sl[st, b, cb] = v.astype(BF)

            @pl.when(st == JOIN)
            def _():
                away_copy(b, cb).wait_recv()
                sl[st, b, cb] = (v + rel[b, cb].astype(F32)).astype(BF)
            near_copy(st, b, cb).start()
        run(4 * n, near, lambda st, cb: 1 + 2 * lax.rem(st + cb, 2), near_on)

        def home(m):
            return HOME, 1 - m // n, lo + lax.rem(m, n)

        def home_on(st, b, cb, v):
            sl[st, b, cb] = v.astype(BF)
        run(2 * n, home, lambda st, cb: 0, home_on)

    def t_copy(cb):
        return remote(sl.at[HOME, THEIRS, cb], zt.at[cb], t_s.at[cb], t_r.at[cb], me.partner)

    def total(b, cb):
        for p in range(2):
            local(fin.at[p, b, cb], fin.at[p, b, cb], fin_r.at[p, b, cb]).wait()
        return sl[HOME, b, cb].astype(F32) + fin[0, b, cb].astype(F32) + fin[1, b, cb].astype(F32)

    @timed('theirs')
    def theirs(lo, hi):
        @each(lo, hi)
        def _(cb):
            sl[HOME, THEIRS, cb] = total(THEIRS, cb).astype(BF)
            t_copy(cb).start()

    def swapped(cb):
        slot = cb // per
        return (slot + 1 - 2 * (slot % 2)) * per + cb % per

    @timed('mine')
    def mine(slot):
        @each(0, per)
        def _(n):
            cb = slot * per + n
            z = total(MINE, cb)
            t_copy(swapped(cb)).wait_recv()
            cols = span(me.slots[slot] * per + n, CB)
            y[:, cols] = (x[:, cols].astype(F32) + (z.astype(BF).astype(F32) + zt[swapped(cb)].astype(F32))).astype(BF)

    @each(0, 3)
    def _(g):
        later = (g + 1) // 2
        lo, n = 2 * (g + later), 2 * (2 - later)

        @pl.when(g == 0)
        def _():
            loads[4].wait()
            loads[5].wait()
        for k in range(2):
            @pl.when(g == 1 + k)
            def _(k=k):
                with scope('w%d' % k):
                    to_mate[k].wait_recv()
        stages(lo, n)
        if nxt:
            @pl.when(g == 0)
            def _():
                with scope('passing'):
                    for t, f in zip(to_t, on):
                        t.wait_recv()
                        f.start()
        theirs(lo, lo + n)
    for slot in SLOTS:
        mine(slot)

    with scope('end'):
        @each(0, nb)
        def _(cb):
            t_copy(cb).wait_send()
            for b in SEQS:
                away_copy(b, cb).wait_send()
                for st in (NEAR, JOIN):
                    near_copy(st, b, cb).wait_send()
        for c in to_mate:
            c.wait_send()
        for c in passing:
            c.wait()
        if nxt:
            for c in to_t[:len(on)]:
                c.wait_send()


def back(layer, mesh, x, om, s_o, t_o, weights, last):
    wq, wkv, wg, wu, wo, wd = weights
    mp = mesh.shape['mp']
    tok, d = x.shape
    t, k = om.shape[1:]
    d4 = wo.shape[2]
    nb = d // CB
    unit = (tok, CB)
    nq, nf = wq.shape[2] // 2, wg.shape[2] // 2
    sds = jax.ShapeDtypeStruct
    outs, specs = [sds((tok, d), BF)], [VM]
    args = [x, om, s_o, t_o, wo, wd]
    if not last:
        args += [wq, wg, wu]
        for n in (AHEAD, NT, AHEAD):
            outs += [sds((d4, nq), BF), sds((n, d4, 2 * nf // NT), BF)]
        specs += [ANY] * 6
    npiece = 1 + 2 * NT
    return pl.pallas_call(
        functools.partial(back_kernel, layer, mp // 2, not last), out_shape=outs,
        in_specs=[VM] + [ANY] * (len(args) - 1), out_specs=specs,
        scratch_shapes=[
            pltpu.VMEM((2, t, k), BF), pltpu.VMEM((4, k, d4), BF),
            pltpu.VMEM((4, 2, nb, *unit), BF), pltpu.VMEM((2, nb, *unit), BF), pltpu.VMEM((2, 2, nb, *unit), BF), pltpu.VMEM((nb, *unit), BF),
            pltpu.VMEM((RING, *unit), BF), pltpu.VMEM((LAG + 1, 2 * tok, CB), F32),
            DMA((6,)), DMA((2,)), DMA((2,)), DMA((3, npiece)), DMA((3, npiece)), DMA((RING,)), DMA((4, 2, nb)),
            DMA((2, nb)), DMA((2, nb)), DMA((2, 2, nb)), DMA((2, 2, nb)), DMA((nb,)), DMA((nb,))],
        compiler_params=pltpu.CompilerParams(vmem_limit_bytes=VMEM_LIMIT, collective_id=2 * layer + 1, has_side_effects=True),
        cost_estimate=pl.CostEstimate(flops=4 * t * k * d, bytes_accessed=2 * (2 * t * k + 4 * k * d4), transcendentals=0),
        name=f"back{layer}")(*args)


def solution(mesh):
    assert mesh.shape['dp'] == len(SLOTS)

    def body(x, lengths, gamma, *weights):
        layers = gamma.shape[0]
        assert layers == 2
        x = x[0]
        gam = jnp.zeros((8, gamma.shape[1]), F32).at[:layers].set(gamma.astype(F32))
        lens = jnp.broadcast_to(lengths.astype(F32)[:, None], (8, 128))
        om, _, s_o, t_o, wkvb, gam, lens = front(0, mesh, x, gam, lens, weights, ())
        x, *ahead = back(0, mesh, x, om, s_o, t_o, weights, False)
        om, _, s_o, t_o = front(1, mesh, x, gam, lens, weights, (wkvb, *ahead))
        (x,) = back(1, mesh, x, om, s_o, t_o, weights, True)
        return x[None]

    in_specs = (P(('rep', 'dp'), 'mp', None), P(('rep', 'dp')), P(None, 'dp'),
                P(None, 'dp', 'mp'), P(None, 'dp', None), P(None, 'dp', 'mp'),
                P(None, 'dp', 'mp'), P(None, 'mp', 'dp'), P(None, 'mp', 'dp'))
    return jax.shard_map(body, mesh=mesh, in_specs=in_specs,
                         out_specs=P(('rep', 'dp'), 'mp', None), check_vma=False)
```

time: 1690 us -> 810 us (0.48)
  waiting for transfers between devices: 912 us -> 0 us
  Pallas kernels: 0 us -> 804 us
  matrix products: 534 us -> 0 us
  local copies, waits for them, and re-layouts: 92.7 us -> 3.73 us
  loops' own time: 64.3 us -> 0 us
  other arithmetic: 41 us -> 1.31 us
  blocking collectives: 20.8 us -> 0 us
    pallas_call x0 -> x4, Pallas kernels: none -> 804 us  [the longest x2 494 us: front(): pl.pallas_call(functools.partial(front_kernel, layer, chips), out_shape=o...]
    all_gather x14 -> x0, waiting for transfers between devices: 737 us -> none  [the longest x2 224 us: layer(): wg = lax.all_gather(wg, 'dp', axis=0, tiled=True)]
    dot_general x44 -> x0, matrix products: 423 us -> none  [the longest x8 225 us: proj(): return jnp.einsum('btd,de->bte', h, w, preferred_element_type=jnp.float32)]
    reduce_scatter x2 -> x0, waiting for transfers between devices: 170 us -> none  [layer(): lax.psum_scatter(z.astype(jnp.bfloat16), 'mp', scatter_dimension=1, tiled...]
    sub x32 -> x0, matrix products: 111 us -> none  [blk(): p = jax.nn.softmax(s, axis=-1).astype(jnp.bfloat16)]
    another operation x2 -> x0, loops' own time: 64.3 us -> none  [attend(): o = lax.map(blk, (qs, jnp.arange(nb * nblk)))]
    dynamic_slice x64 -> x0, local copies, waits for them, and re-layouts: 52.6 us -> none  [attend(): o = lax.map(blk, (qs, jnp.arange(nb * nblk)))]
    slice x9 -> x0, local copies, waits for them, and re-layouts: 28.8 us -> none  [the longest x7 26.5 us: body(): x = layer(x, lengths, gamma[l], wq[l], wkv[l], wg[l], wu[l], wo[l], wd[l])]
  transfers between devices with their start and end apart: 16 -> 0, of which waited for: 14 -> 0; matrix products, arithmetic and copies ran while one was open for 34% -> 0% of each run, Pallas kernels for 0% -> 0%
where the time goes in v1:
time: 810 us
  Pallas kernels  804 us (99%)
    pallas_call x2, Pallas kernels, front(): pl.pallas_call(functools.partial(front_kernel, layer, chips), out_shape=o...  494 us
    pallas_call x2, Pallas kernels, back(): pl.pallas_call(functools.partial(back_kernel, layer, mp // 2, not last),...  309 us

profile of v1, /device:TPU:97, one launch (start us, length us, event | category | flops | bytes accessed | tf_op | source)
XLA Modules:
  0.0 809.5 jit_solution(1967497598032054118)
XLA Ops:
  0.7 0.6 broadcast_in_dim.13.refs_2_
  1.3 1.3 pad_convert_fusion.refs_1_
  2.6 274.9 %front0.1 = (bf16[2,2048,1280]{2,1,0:T(8,128)(2,1)}, bf16[2,2048,4096]{2,1,0:T(8,128)(2,1)}, bf16[768,1024]{1,0:T(8,128)(2,1)}, bf16[1280,1024]{1,0:T(8,128)(2,1...) custom-call(bf16[256,4096]{1,0:T(8,128)(2,1)} %bitcast.4, ...), custom_call_target="tpu_custom_call" | custom-call | flops 94489280512 | bytes 100663296 | tf_op jit(solution)/shard_map/front0/pallas_call | solution.py:635
  277.5 155.0 %back0.1 = (bf16[256,4096]{1,0:T(8,128)(2,1)}, bf16[1024,256]{1,0:T(8,128)(2,1)}, bf16[1,1024,512]{2,1,0:T(8,128)(2,1)}, bf16[1024,256]{1,0:T(8,128)(2,1)}, bf16...) custom-call(bf16[256,4096]{1,0:T(8,128)(2,1)} %bitcast.5, ...), custom_call_target="tpu_custom_call" | custom-call | flops 42949672960 | bytes 20971520 | tf_op jit(solution)/shard_map/back0/pallas_call | solution.py:864
  432.4 219.6 %front1.1 = (bf16[2,2048,1280]{2,1,0:T(8,128)(2,1)}, bf16[2,2048,4096]{2,1,0:T(8,128)(2,1)}, bf16[768,1024]{1,0:T(8,128)(2,1)}, bf16[1280,1024]{1,0:T(8,128)(2,1)}) custom-call(bf16[256,4096]{1,0:T(8,128)(2,1)} %get-tuple-element.36.refs_0_, f32[4,8,1024]{2,1,0:T(8,128)} %get-tuple-element.37.refs_1_, f32[2,8,128]{2,1,0:T(8,128)} %get-tuple-element.38.refs_2_, ...), custom_call_target="tpu_custom_call" | custom-call | flops 94489280512 | bytes 100663296 | tf_op jit(solution)/shard_map/front1/pallas_call | solution.py:635
  652.0 154.4 %back1.1 = bf16[256,4096]{1,0:T(8,128)(2,1)} custom-call(bf16[256,4096]{1,0:T(8,128)(2,1)} %get-tuple-element.36.refs_0_, bf16[2,2048,1280]{2,1,0:T(8,128)(2,1)} %get-tuple-element.46.refs_1_, bf16[768,1024]{1,0:T(8,128)(2,1)} %get-tuple-element.47.refs_2_, bf16[1280,1024]{1,0:T(8,128)(2,1)} %get-tuple-element.48.refs_3_, bf16[2,512,1024]{2,1,0:T(8,128)(2,1)} %refs_4_.7, ...), custom_call_target="tpu_custom_call" | custom-call | flops 42949672960 | bytes 20971520 | tf_op jit(solution)/shard_map/back1/pallas_call | solution.py:864
  806.4 3.1 copy.12

commit v2 on v1

--- a/solution.py
+++ b/solution.py
@@ -16,10 +16,13 @@
 NT = 4
 CB = 512
 RING, LAG = 4, 2
+LANES = 128
+BLOCK = 512
 VMEM_LIMIT = 63 * 2**20
 
 OWN, PART, MATE, FAR = SLOTS = range(4)
 S, T, F = KINDS = range(3)
+KIND_OF = {MATE: S, PART: T, FAR: F}
 GATE, UP = GU = range(2)
 MINE, THEIRS = SEQS = range(2)
 
@@ -58,14 +61,16 @@
 
 
 class Place:
-    def __init__(self, chips):
+    def __init__(self, chips, layer):
         self.chips = chips
         self.r = lax.axis_index('dp')
         self.j = lax.axis_index('mp')
         self.chip, self.core = self.j // 2, self.j % 2
-        mate = self.r + 1 - 2 * (self.r % 2)
-        self.slots = (self.r, 3 - self.r, mate, lax.rem(self.r + 2, 4))
-        self.half = self.r // 2
+        sides = 3 - self.r, self.r + 1 - 2 * (self.r % 2)
+        odd = layer % 2
+        self.slots = (self.r, sides[odd], sides[1 - odd], lax.rem(self.r + 2, 4))
+        self.half = lax.rem((self.r + odd) // 2, 2)
+        self.named = (OWN, MATE, PART, FAR) if odd else SLOTS
         self.partner, self.mate, self.across = ({'dp': s} for s in self.slots[1:])
         self.sib = {'mp': self.chip * 2 + 1 - self.core}
         self.next, self.prev = self.at(1), self.at(chips - 1)
@@ -106,7 +111,7 @@
 
 
 def split_rows(o, n):
-    return [o.at[pl.ds(0, n), :], o.at[pl.ds(n, o.shape[0] - n), :]]
+    return [o.at[pl.ds(0, n), :]] + ([o.at[pl.ds(n, o.shape[0] - n), :]] if n < o.shape[0] else [])
 
 
 def front_kernel(layer, chips, *refs):
@@ -115,14 +120,14 @@
     take = lambda n: [next(it) for _ in range(n)]
     x, gam, lens, wq, wkv, wg, wu, wo, wd = take(9)
     if first:
-        om, hbuf, s_o, t_o, wkvb, gb, lenb = take(7)
+        om, hbuf, s_o, t_o, sg1, wkvb, gb, lenb = take(8)
     else:
-        wkvb, sq, sg, tq, tg, fq, fg = take(7)
+        sg1, wkvb, *ahead = take(8)
         om, hbuf, s_o, t_o = take(4)
         gb, lenb = gam, lens
     (wqkv, wgu, hv, qkv, hown, hpar, wkvp, sc, ms, os, y_s, y_r, ld, o_s, o_r, kv_sem, hv_sem, ms_sem, os_sem, ag_s, ag_r, own_sem,
      ex_s, ex_r) = it
-    me = Place(chips)
+    me = Place(chips, layer)
     pc = Pieces(layer, wq, wg, wu, me)
     mp = 2 * chips
     tok, d4, nq = x.shape[0], wq.shape[1], pc.nq
@@ -136,28 +141,31 @@
     def raw(half, which, t):
         return pc.q(half) if which < GATE else pc.g(half, which, t)
 
-    def given(q, g, which, t):
-        return q if which < GATE else pc.tile_part(g.at[t], which)
+    def given(kind, which, t):
+        q, g = ahead[2 * kind:2 * kind + 2]
+        if which < GATE:
+            return q
+        return pc.tile_part(sg1 if kind == S and t == EARLY else g.at[t], which)
 
     def sem(which, t):
         return 0 if which < GATE else 1 + 2 * t + which
 
     def load(s, which, t):
-        n = sem(which, t)
-        if s == OWN:
-            src = raw(me.half, which, t)
-        else:
-            src = given(*{MATE: (sq, sg), PART: (tq, tg), FAR: (fq, fg)}[s] if not first else (), which, t)
-        return local(src, at_slot(s, which, t), ld.at[s, n])
+        src = raw(me.half, which, t) if s == OWN else given(KIND_OF[s], which, t)
+        return local(src, at_slot(s, which, t), ld.at[s, sem(which, t)])
+
+    def came(kind, t):
+        return not first and (t is None or (isinstance(t, int) and (t < AHEAD[kind] or (kind == S and t == EARLY))))
 
     def move(kind, which, t):
         n = sem(which, t)
+        sems = (y_s.at[kind, n], y_r.at[kind, n])
         if kind == S:
-            return remote(raw(me.half, which, t), at_slot(MATE, which, t), y_s.at[S, n], y_r.at[S, n], me.mate)
+            return remote(raw(me.half, which, t), at_slot(MATE, which, t), *sems, me.mate)
         if kind == T:
-            return remote(raw(1 - me.half, which, t), at_slot(PART, which, t), y_s.at[T, n], y_r.at[T, n], me.partner)
-        src = at_slot(PART, which, t) if first else given(tq, tg, which, t)
-        return remote(src, at_slot(FAR, which, t), y_s.at[F, n], y_r.at[F, n], me.mate)
+            return remote(raw(1 - me.half, which, t), at_slot(PART, which, t), *sems, me.partner)
+        src = given(T, which, t) if came(T, None if which < GATE else t) else at_slot(PART, which, t)
+        return remote(src, at_slot(FAR, which, t), *sems, me.mate)
 
     def parts(t):
         return [(GATE - 1, 0)] if t is None else [(w, t) for w in GU]
@@ -171,36 +179,33 @@
     def relay(*ts):
         for t in ts:
             for p in parts(t):
-                if first:
+                if not came(T, t):
                     move(T, *p).wait_recv()
                 move(F, *p).start()
-
-    def sent_ahead(t):
-        return not first and (t is None or (isinstance(t, int) and t < AHEAD))
 
     @timed('have')
     def have(*ts):
         for t in ts:
             for p in parts(t):
                 load(OWN, *p).wait()
-                if sent_ahead(t):
+                if came(S, t):
                     load(MATE, *p).wait()
+                else:
+                    move(S, *p).wait_recv()
+                if came(T, t):
+                    load(PART, *p).wait()
+                if came(F, t):
                     load(FAR, *p).wait()
                 else:
-                    move(S, *p).wait_recv()
                     move(F, *p).wait_recv()
-                if not first:
-                    load(PART, *p).wait()
 
     every = [None, *range(NT)]
     for t in every:
         for p in parts(t):
             load(OWN, *p).start()
-            if not first:
-                load(PART, *p).start()
-            if sent_ahead(t):
-                load(MATE, *p).start()
-                load(FAR, *p).start()
+            for s, kind in KIND_OF.items():
+                if came(kind, t):
+                    load(s, *p).start()
 
     with scope('meet'):
         me.meet(me.sib, me.next, me.prev, me.mate, me.partner, *([me.across] if first else []))
@@ -210,6 +215,11 @@
     ahead_o = zip(oth_o + [own_o[0], own_o[1].at[pl.ds(0, s_o.shape[0] - no), :]], split_rows(t_o, no) + split_rows(s_o, no),
                   [me.partner, me.partner, me.mate, me.mate])
     out_moves = [remote(src, dst, o_s.at[n], o_r.at[n], dev) for n, (src, dst, dev) in enumerate(ahead_o)]
+
+    if first:
+        then = Place(chips, layer + 1)
+        pn = Pieces(layer + 1, wq, wg, wu, then)
+        out_moves += [remote(pn.g(then.half, which, EARLY), pc.tile_part(sg1, which), o_s.at[4 + which], o_r.at[4 + which], then.mate) for which in GU]
 
     small = []
     if first:
@@ -217,11 +227,12 @@
         kv_own.start()
         for s, dev in ((PART, me.partner), (MATE, me.mate), (FAR, me.across)):
             small.append(remote(gam, gb.at[s], ex_s.at[s], ex_r.at[s], dev))
-        small.append(remote(lens, lenb.at[THEIRS], ex_s.at[OWN], ex_r.at[OWN], me.partner))
+        for s, dev in ((PART, me.partner), (MATE, me.mate)):
+            small.append(remote(lens, lenb.at[s], ex_s.at[7 + s], ex_r.at[7 + s], dev))
         for c in small:
             c.start()
         gb[OWN] = gam[:, :]
-        lenb[MINE] = lens[:, :]
+        lenb[OWN] = lens[:, :]
         kv_own.wait()
 
         def kv_move(kind):
@@ -229,15 +240,13 @@
             return remote(wkvp.at[:, src], wkvp.at[:, dst], ex_s.at[4 + kind], ex_r.at[4 + kind], dev)
         for k in (T, S):
             kv_move(k).start()
-            send(k, None)
-        send(T, 0)
+            send(k, 0)
         with scope('small'):
             for c in small:
                 c.wait_recv()
     else:
-        for t in range(1, NT):
-            send(S, t)
-            relay(t)
+        relay(1)
+        send(S, 2, 3)
 
     @timed('norm')
     def norm():
@@ -252,7 +261,7 @@
             rstd = lax.rsqrt(jnp.mean(xc * xc, axis=-1, keepdims=True) + EPS)
             for s in SLOTS:
                 cols = span(me.slots[s], d4)
-                hown[rows, cols] = ((x[rows, cols].astype(F32) - mu) * rstd * gb[s, layer:layer + 1, :]).astype(BF)
+                hown[rows, cols] = ((x[rows, cols].astype(F32) - mu) * rstd * gb[me.named[s], layer:layer + 1, :]).astype(BF)
     norm()
 
     SIB, TO, SHARE, PASS, LAST = range(5)
@@ -338,39 +347,39 @@
         return span(me.chip_at(i + i // 2 - 2 * (i // 3)), rows2)
 
     def hload(i):
-        return local(hbuf.at[i // 4, chip_rows(lax.rem(i, 4)), :], hv.at[lax.rem(i, 2)], hv_sem.at[lax.rem(i, 2)])
-
-    def hdot(buf, w):
+        return local(hbuf.at[i // chips, chip_rows(lax.rem(i, chips)), :], hv.at[lax.rem(i, 2), pl.ds(0, rows2), :], hv_sem.at[lax.rem(i, 2)])
+
+    def hdot(i, rows, w):
         acc = None
         for s in SLOTS:
-            p = dot(hv[buf, :, span(me.slots[s], d4)], w(s))
+            p = dot(hv[lax.rem(i, 2), :rows, span(me.slots[s], d4)], w(s))
             acc = p if acc is None else acc + p
         return acc
 
-    def mcopy(i, t, k):
+    def mcopy(b, rows, n, t, k):
         w = pc.tile
-        return local(ms.at[k], om.at[i // 4, chip_rows(lax.rem(i, 4)), pl.ds(pl.multiple_of(nq + t * w, w), w)], ms_sem.at[k])
-
-    def tile(i, t, m):
+        return local(ms.at[k, pl.ds(0, n), :], om.at[b, rows, pl.ds(pl.multiple_of(nq + t * w, w), w)], ms_sem.at[k])
+
+    def tile(i, b, rows, n, t, m):
         k = lax.rem(m, 2)
-        a = hdot(lax.rem(i, 2), lambda s: wgu[s, t])
+        a = hdot(i, n, lambda s: wgu[s, t])
 
         @pl.when(m >= 2)
         def _():
-            mcopy(i, t, k).wait()
+            mcopy(b, rows, n, t, k).wait()
         gt = a[:, :pc.tile].astype(BF).astype(F32)
         up = a[:, pc.tile:].astype(BF).astype(F32)
-        ms[k] = (gt * jax.nn.sigmoid(gt) * up).astype(BF)
-        mcopy(i, t, k).start()
-
-    def drain():
+        ms[k, :n, :] = (gt * jax.nn.sigmoid(gt) * up).astype(BF)
+        mcopy(b, rows, n, t, k).start()
+
+    def drain(n):
         for k in range(2):
-            mcopy(0, 0, k).wait()
+            mcopy(MINE, pl.ds(0, n), n, 0, k).wait()
 
     def any_of(i, marks):
         return functools.reduce(lambda a, b: a | b, [i == g for g in marks])
 
-    def sweep(b, nt, gates, hooks):
+    def sweep(b, qk, nt, gates, hooks):
         lo = b * chips
         marks = [n for n in gates]
 
@@ -387,33 +396,52 @@
             def _():
                 hload(i + 1).start()
             hload(i).wait()
-            qkv[b, chip_rows(i - lo), :] = hdot(lax.rem(i, 2), lambda s: wqkv[s]).astype(BF)
+            rows = chip_rows(i - lo)
+            if qk:
+                qkv[b, rows, :] = hdot(i, rows2, lambda s: wqkv[s]).astype(BF)
 
             @each(0, nt)
             def _(t):
                 for n, f in hooks.items():
                     pl.when((i == lo) & (b == MINE) & (t == n))(f)
-                tile(i, t, (i - lo) * nt + t)
-        drain()
-
-    def late(lo_t, hi_t, lo, hi):
-        n = hi - lo
-        hload(lo).start()
-
-        @each(0, n * (hi_t - lo_t))
-        def _(u):
-            i, t = lo + lax.rem(u, n), lo_t + u // n
+                tile(i, b, rows, rows2, t, (i - lo) * nt + t)
+
+        @pl.when(nt + lo >= 1)
+        def _():
+            drain(rows2)
+
+    def late(lo_t, hi_t, lo, hi, hooks):
+        big = hv.shape[1]
+        per = qkv.shape[1] // big
+        n = (hi - lo) * per
+
+        def place(u):
+            v = lo * per + lax.rem(u, n)
+            return v // per, span(lax.rem(v, per), big)
+
+        def load_big(u):
+            b, rows = place(u)
+            return local(hbuf.at[b, rows, :], hv.at[lax.rem(u, 2)], hv_sem.at[lax.rem(u, 2)])
+
+        def run():
+          @each(0, n * (hi_t - lo_t))
+          def _(u):
+            t = lo_t if hi_t - lo_t == 1 else lo_t + u // n
 
             @pl.when(lax.rem(u, n) == 0)
             def _():
                 have(t)
+            for k, f in hooks.items():
+                pl.when(u == k)(f)
 
             @pl.when(u + 1 < n * (hi_t - lo_t))
             def _():
-                hload(lo + lax.rem(u + 1, n)).start()
-            hload(i).wait()
-            tile(i, t, u)
-        drain()
+                load_big(u + 1).start()
+            load_big(u).wait()
+            b, rows = place(u)
+            tile(u, b, rows, big, t, u)
+          drain(big)
+        return load_big(0).start, run
 
     bq, bk = sc.shape[1:]
 
@@ -426,13 +454,12 @@
             return local(os.at[k], om.at[b, span(i, bq), pl.ds(0, dh)], os_sem.at[k])
 
         def lanes(a, op):
-            w = a.shape[1] // ratio // 2
-            return functools.reduce(op, [a[:, n * w:(n + 1) * w] for n in range(2 * ratio)])
+            return functools.reduce(op, [a[:, n * LANES:(n + 1) * LANES] for n in range(bk // LANES)])
 
         @each(0, nblk)
         def _(i):
             q = qkv[b, span(i, bq), pl.ds(0, dh)]
-            length = lenb[b, :, :][:1, :1]
+            length = lenb[b * me.named[PART], :, :][:1, :1]
             colf = lax.broadcasted_iota(jnp.int32, (1, bk), 1).astype(F32)
 
             def raw_score(j):
@@ -458,7 +485,7 @@
                 sc[j] = p
                 return l + lanes(p, jnp.add)
 
-            l = jnp.sum(lax.fori_loop(0, last + 1, expo, jnp.zeros((bq, bk // ratio // 2), F32)), axis=1, keepdims=True)
+            l = jnp.sum(lax.fori_loop(0, last + 1, expo, jnp.zeros((bq, LANES), F32)), axis=1, keepdims=True)
             inv = 1.0 / l
 
             def value(j, o):
@@ -477,7 +504,8 @@
 
     def kv_load(u):
         s, j = u // mp, lax.rem(u, mp)
-        return local(wkvb.at[layer, j, s], wqkv.at[s, span(j, wkvp.shape[2]), pl.ds(nq, 2 * dh)], kv_sem.at[u])
+        name = s if first else s + (1 - s // 3) * (s - s // 2 * 2 - s // 2 * 1)
+        return local(wkvb.at[layer, j, s], wqkv.at[name, span(j, wkvp.shape[2]), pl.ds(nq, 2 * dh)], kv_sem.at[u])
 
     def kv_loads(go):
         @each(0, 4 * mp)
@@ -508,95 +536,112 @@
         gb2.own()
 
     ga.own()
-    ht.start()
     if first:
         with scope('kvmove'):
             kv_move(T).wait_recv()
             kv_move(F).start()
+        send(T, None)
+        with scope('kvmove2'):
             kv_move(S).wait_recv()
-        send(S, 0)
-        send(T, 1)
-        relay(None)
-        send(S, 1)
-        with scope('kvmove2'):
             kv_move(F).wait_recv()
         gw = [gather(2 + n, wkvp.at[n], lambda j, n=n: wkvb.at[n, j], lambda ref, k: ref.at[pl.ds(2 * k, 2)]) for n in range(2)]
         relay(0)
+        send(S, None)
+        ht.start()
+        relay(None)
+        ga.near()
+        gw[0].own()
+        for kind in (SIB, SHARE):
+            ga.has(kind)
+        have(0)
+        send(S, 1)
+        send(T, 1)
         send(S, 2)
+
+        def far_a():
+            ga.far()
+            ga.has(LAST)
+        with scope('pre'):
+            sweep(MINE, False, 1, {3: far_a}, {})
+        gw[0].near()
+        start_b()
         send(T, 2)
         send(T, 3)
-        ga.near()
-        gw[0].own()
+        gw[0].far()
         for c in out_moves[:2]:
             c.start()
-        ga.far()
-        gw[0].near()
-        start_b()
-        gw[0].far()
-        gw[1].own()
         for kind in (SIB, SHARE, LAST):
             gw[0].has(kind)
         kv_loads(lambda c: c.start())
-        for kind in (SIB, SHARE, LAST):
-            ga.has(kind)
         kv_loads(lambda c: c.wait())
-        have(None, 0)
+        have(None)
+        load_late, run_late = late(1, NT, MINE, len(SEQS), {4: gw[1].near, 8: gw[1].far})
 
         @each(0, 2)
         def _(b):
             with scope('sweep'):
-                sweep(b, 1, {chips: both(lambda: gb2.has(SIB), gb2.near), chips + 1: both(lambda: gb2.has(SHARE), gw[1].near),
-                             chips + 3: both(far_of(gb2), gw[1].far)}, {})
+                sweep(b, True, b, {chips: lambda: gb2.has(SIB), chips + 1: both(near_of(gb2), lambda: relay(2)),
+                                   chips + 3: far_of(gb2)}, {})
 
             @pl.when(b == MINE)
             def _():
                 relay(1)
                 send(S, 3)
-            attend(b)
-
-            @pl.when(b == MINE)
-            def _():
-                relay(2)
 
             @pl.when(b == THEIRS)
             def _():
                 relay(3)
                 for c in out_moves[2:]:
                     c.start()
+                gw[1].own()
+                load_late()
+            attend(b)
+
         with scope('late'):
-            late(1, NT, 0, 2 * chips)
+            run_late()
         for kind in (SIB, SHARE, LAST):
             gw[1].has(kind)
     else:
-        for c in out_moves:
+        ht.start()
+        send(T, 2, 3)
+        for c in out_moves[:2]:
             c.start()
         kv_loads(lambda c: c.start())
         kv_loads(lambda c: c.wait())
         have(None, 0)
 
+        def far_a():
+            far_of(ga)()
+            relay(2)
+        load_some, run_some = late(2, 3, MINE, THEIRS, {})
+        load_late, run_late = late(3, NT, MINE, len(SEQS), {})
+
         @each(0, 2)
         def _(b):
             with scope('sweep'):
-                sweep(b, 2 + b, {0: lambda: ga.has(SIB), 1: both(near_of(ga), start_b), 3: far_of(ga),
-                                 chips: both(lambda: gb2.has(SIB), gb2.near), chips + 1: lambda: gb2.has(SHARE), chips + 3: far_of(gb2)},
+                sweep(b, True, 2 + b, {0: lambda: ga.has(SIB), 1: both(near_of(ga), start_b), 3: far_a,
+                                       chips: both(lambda: gb2.has(SIB), gb2.near), chips + 1: lambda: gb2.has(SHARE), chips + 3: far_of(gb2)},
                       {1: lambda: have(1)})
+            pl.when(b == MINE)(load_some)
+            pl.when(b == THEIRS)(load_late)
             attend(b)
 
             @pl.when(b == MINE)
             def _():
+                relay(3)
+                for c in out_moves[2:]:
+                    c.start()
                 with scope('late2'):
-                    late(2, 3, 0, chips)
+                    run_some()
         with scope('late'):
-            late(3, NT, 0, 2 * chips)
+            run_late()
 
     with scope('end'):
         for t in every:
             for p in parts(t):
-                if not sent_ahead(t):
-                    move(S, *p).wait_send()
-                    move(F, *p).wait_send()
-                if first:
-                    move(T, *p).wait_send()
+                for k in KINDS:
+                    if not came(k, t):
+                        move(k, *p).wait_send()
         for c in out_moves:
             c.wait()
         ht.wait_send()
@@ -611,7 +656,8 @@
                 kv_move(k).wait_send()
 
 
-AHEAD = 1
+EARLY = 1
+AHEAD = (1, 2, 1)
 
 
 def front(layer, mesh, x, gam, lens, weights, given):
@@ -626,22 +672,22 @@
     t = tok * mp
     kvr = wkv.shape[1] // mp
     sds = jax.ShapeDtypeStruct
-    outs = [sds((2, t, nq + nf), BF), sds((2, t, d), BF), sds((no + nd // 2, d4), BF), sds((no + nd, d4), BF)]
+    outs = [sds((2, t, nq + nf), BF), sds((2, t, d), BF), sds((no + (nd // 2 if first else nd), d4), BF), sds((no + nd, d4), BF)]
     specs = [ANY] * 4
     if first:
-        outs += [sds((2, mp, 4, kvr, nkv), BF), sds((4, *gam.shape), F32), sds((2, *lens.shape), F32)]
-        specs += [ANY, VM, VM]
+        outs += [sds((d4, 2 * nf // NT), BF), sds((2, mp, 4, kvr, nkv), BF), sds((4, *gam.shape), F32), sds((3, *lens.shape), F32)]
+        specs += [ANY, ANY, VM, VM]
     npiece = 1 + 2 * NT
     return pl.pallas_call(
         functools.partial(front_kernel, layer, chips), out_shape=outs,
         in_specs=[VM, VM, VM] + [ANY] * (6 + len(given)), out_specs=specs,
         scratch_shapes=[
-            pltpu.VMEM((4, d4, nq + nkv), BF), pltpu.VMEM((4, NT, d4, 2 * nf // NT), BF), pltpu.VMEM((2, 2 * tok, d), BF),
+            pltpu.VMEM((4, d4, nq + nkv), BF), pltpu.VMEM((4, NT, d4, 2 * nf // NT), BF), pltpu.VMEM((2, 4 * tok, d), BF),
             pltpu.VMEM((2, t, nq + nkv), BF), pltpu.VMEM((tok, d), BF), pltpu.VMEM((tok, d), BF),
-            pltpu.VMEM((2, 4, kvr, nkv), BF), pltpu.VMEM((t // nq // 2, nq, 2 * nq), F32),
-            pltpu.VMEM((2, 2 * tok, nf // NT), BF), pltpu.VMEM((2, nq, nq), BF),
-            DMA((3, npiece)), DMA((3, npiece)), DMA((4, npiece)), DMA((4,)), DMA((4,)), DMA((4 * mp,)), DMA((2,)), DMA((2,)), DMA((2,)),
-            DMA((4, 20)), DMA((4, 20)), DMA((5,)), DMA((8,)), DMA((8,))],
+            pltpu.VMEM((2, 4, kvr, nkv), BF), pltpu.VMEM((t // BLOCK, BLOCK, BLOCK), F32),
+            pltpu.VMEM((2, 4 * tok, nf // NT), BF), pltpu.VMEM((2, BLOCK, nq), BF),
+            DMA((3, npiece)), DMA((3, npiece)), DMA((4, npiece)), DMA((6,)), DMA((6,)), DMA((4 * mp,)), DMA((2,)), DMA((2,)), DMA((2,)),
+            DMA((4, 20)), DMA((4, 20)), DMA((5,)), DMA((10,)), DMA((10,))],
         compiler_params=pltpu.CompilerParams(vmem_limit_bytes=VMEM_LIMIT, collective_id=2 * layer, has_side_effects=True),
         cost_estimate=pl.CostEstimate(flops=4 * t * d * (nq + nkv + 2 * nf), bytes_accessed=12 * t * d, transcendentals=0),
         name=f"front{layer}")(x, gam, lens, *weights, *given)
@@ -655,9 +701,9 @@
         wq, wg, wu = take(3)
     y = next(it)
     if nxt:
-        sq, sg, tq, tg, fq, fg = take(6)
+        bufs = take(6)
     (om, w, sl, rel, fin, zt, sib, acc, in_sem, w_s, w_r, p_s, p_r, sib_s, sib_r, rel_s, rel_r, fin_s, fin_r, t_s, t_r) = it
-    me = Place(chips)
+    me = Place(chips, layer)
     nb, rows = zt.shape[:2]
     per = w.shape[2] // CB
     no, ns = wo.shape[1] // 2, s_o.shape[0]
@@ -667,28 +713,34 @@
     loads = [local(om_h.at[THEIRS], om.at[THEIRS], in_sem.at[0]), local(own_o[0], own_rows[0], in_sem.at[1]),
              local(own_o[1], own_rows[1], in_sem.at[2]), local(t_o, w.at[PART], in_sem.at[3]), local(om_h.at[MINE], om.at[MINE], in_sem.at[4]),
              local(s_o, mate_rows[0], in_sem.at[5])]
-    for c in loads:
+    for c in loads[:3]:
         c.start()
     me.meet(me.sib, me.next, me.prev, me.mate, me.partner)
-    to_mate = [remote(own_o[1].at[pl.ds(ns - no, no + own_o[1].shape[0] - ns), :], mate_rows[1], w_s.at[0], w_r.at[0], me.mate), remote(t_o, w.at[FAR], w_s.at[1], w_r.at[1], me.mate)]
-    for c in to_mate:
+    for c in loads[3:]:
         c.start()
+    to_mate = [remote(t_o.at[:, span(n, CB)], w.at[FAR, :, span(n, CB)], w_s.at[n], w_r.at[n], me.mate) for n in range(per)]
+    if nxt:
+        to_mate.insert(0, remote(own_o[1].at[pl.ds(ns - no, no + own_o[1].shape[0] - ns), :], mate_rows[1], w_s.at[per], w_r.at[per], me.mate))
+    else:
+        for c in to_mate:
+            c.start()
     passing = []
     if nxt:
-        pc = Pieces(layer + 1, wq, wg, wu, me)
-
-        def buffers(q, g, nt):
-            return [q] + [pc.tile_part(g.at[t], which) for t in range(nt) for which in GU]
-
-        def args(half, nt):
-            return [pc.q(half)] + [pc.g(half, which, t) for t in range(nt) for which in GU]
-
-        def ahead(kind, srcs, dsts, dev):
-            return [remote(*sd, p_s.at[kind, n], p_r.at[kind, n], dev) for n, sd in enumerate(zip(srcs, dsts))]
-        to_s = ahead(S, args(me.half, AHEAD), buffers(sq, sg, AHEAD), me.mate)
-        to_t = ahead(T, args(1 - me.half, NT), buffers(tq, tg, NT), me.partner)
-        on = ahead(F, buffers(tq, tg, AHEAD), buffers(fq, fg, AHEAD), me.mate)
-        for c in to_t + to_s:
+        then = Place(chips, layer + 1)
+        pc = Pieces(layer + 1, wq, wg, wu, then)
+
+        def ahead(kind, dev):
+            q, g = bufs[2 * kind:2 * kind + 2]
+            dst = [q] + [pc.tile_part(g.at[t], which) for t in range(AHEAD[kind]) for which in GU]
+            if kind == F:
+                q, g = bufs[2 * T:2 * T + 2]
+                src = [q] + [pc.tile_part(g.at[t], which) for t in range(AHEAD[F]) for which in GU]
+            else:
+                half = then.half if kind == S else 1 - then.half
+                src = [pc.q(half)] + [pc.g(half, which, t) for t in range(AHEAD[kind]) for which in GU]
+            return [remote(*sd, p_s.at[kind, n], p_r.at[kind, n], dev) for n, sd in enumerate(zip(src, dst))]
+        to_s, to_t, on = ahead(S, then.mate), ahead(T, then.partner), ahead(F, then.mate)
+        for c in (*to_t[:len(on)], *to_mate, *to_s, *to_t[len(on):]):
             c.start()
         passing = to_s + on + to_t[len(on):]
     with scope('loads'):
@@ -737,39 +789,49 @@
                 finish(st, b, cb, combined(st, b, cb, m - LAG))
 
         for m in range(RING):
-            sib_copy(HOME, MINE, 0, m).wait_send()
-
-    @timed('stages')
-    def stages(lo, n):
-        def away(m):
-            return AWAY, 1 - m // n, lo + lax.rem(m, n)
-
-        def away_on(st, b, cb, v):
+            @pl.when(m < n)
+            def _(m=m):
+                sib_copy(HOME, MINE, 0, m).wait_send()
+
+    @timed('depart')
+    def depart(lo, n):
+        def unit(m):
+            return m // (2 * n), 1 - lax.rem(m // n, 2), lo + lax.rem(m, n)
+
+        def off(st, cb):
+            return (1 - st) * 2 + st * (1 + 2 * lax.rem(st + cb, 2))
+
+        def on(st, b, cb, v):
             sl[st, b, cb] = v.astype(BF)
-            away_copy(b, cb).start()
-        run(2 * n, away, lambda st, cb: 2, away_on)
-
-        def near(m):
-            return NEAR + lax.rem(m // n, 2), 1 - m // (2 * n), lo + lax.rem(m, n)
-
-        def near_on(st, b, cb, v):
+
+            @pl.when(st == AWAY)
+            def _():
+                away_copy(b, cb).start()
+
             @pl.when(st == NEAR)
             def _():
-                sl[st, b, cb] = v.astype(BF)
-
+                near_copy(NEAR, b, cb).start()
+        run(4 * n, unit, off, on)
+
+    @timed('join')
+    def join(lo, n):
+        def unit(m):
+            return JOIN + m // (2 * n), 1 - lax.rem(m // n, 2), lo + lax.rem(m, n)
+
+        def off(st, cb):
+            return (HOME - st) * (1 + 2 * lax.rem(st + cb, 2))
+
+        def on(st, b, cb, v):
             @pl.when(st == JOIN)
             def _():
                 away_copy(b, cb).wait_recv()
-                sl[st, b, cb] = (v + rel[b, cb].astype(F32)).astype(BF)
-            near_copy(st, b, cb).start()
-        run(4 * n, near, lambda st, cb: 1 + 2 * lax.rem(st + cb, 2), near_on)
-
-        def home(m):
-            return HOME, 1 - m // n, lo + lax.rem(m, n)
-
-        def home_on(st, b, cb, v):
-            sl[st, b, cb] = v.astype(BF)
-        run(2 * n, home, lambda st, cb: 0, home_on)
+                sl[JOIN, b, cb] = (v + rel[b, cb].astype(F32)).astype(BF)
+                near_copy(JOIN, b, cb).start()
+
+            @pl.when(st == HOME)
+            def _():
+                sl[HOME, b, cb] = v.astype(BF)
+        run(4 * n, unit, off, on)
 
     def t_copy(cb):
         return remote(sl.at[HOME, THEIRS, cb], zt.at[cb], t_s.at[cb], t_r.at[cb], me.partner)
@@ -790,41 +852,128 @@
         slot = cb // per
         return (slot + 1 - 2 * (slot % 2)) * per + cb % per
 
+    def give_copy(st, cb):
+        if st == HOME:
+            return t_copy(cb)
+        if st == AWAY:
+            dst, *sems = rel.at[THEIRS, cb], rel_s.at[THEIRS, cb], rel_r.at[THEIRS, cb]
+        else:
+            p = st - NEAR
+            dst, *sems = fin.at[p, THEIRS, cb], fin_s.at[p, THEIRS, cb], fin_r.at[p, THEIRS, cb]
+        return remote(sl.at[st, THEIRS, cb], dst, *sems, me.partner)
+
+    def given(st, cb):
+        c = swapped(cb)
+        give_copy(st, c).wait_recv()
+        return (rel[THEIRS, c] if st == AWAY else zt[c] if st == HOME else fin[st - NEAR, THEIRS, c]).astype(F32)
+
+    def offset(st, cb):
+        first, home = (HOME - st) // HOME, st // HOME
+        return 2 * first + (1 - first) * (1 - home) * (1 + 2 * lax.rem(st + cb, 2))
+
+    @timed('give')
+    def give(lo, n):
+        def unit(m):
+            return lax.rem(m, 4), THEIRS, swapped(lo + m // 4)
+
+        def on(st, b, cb, v):
+            sl[st, THEIRS, cb] = v.astype(BF)
+            for k in (AWAY, NEAR, JOIN, HOME):
+                @pl.when(st == k)
+                def _(k=k):
+                    give_copy(k, cb).start()
+        run(4 * n, unit, offset, on)
+
+    @timed('take')
+    def take(lo, n):
+        def unit(m):
+            k = lax.rem(m, 4)
+            return k + k // 2 - 2 * (k // 3), MINE, lo + m // 4
+
+        def on(st, b, cb, v):
+            for k in (AWAY, NEAR, JOIN, HOME):
+                @pl.when(st == k)
+                def _(k=k):
+                    z = v + given(k, cb)
+                    if k == JOIN:
+                        away_copy(MINE, cb).wait_recv()
+                        z = z + rel[MINE, cb].astype(F32)
+                    sl[k, MINE, cb] = z.astype(BF)
+                    if k == AWAY:
+                        away_copy(MINE, cb).start()
+                    elif k != HOME:
+                        near_copy(k, MINE, cb).start()
+        run(4 * n, unit, offset, on)
+
     @timed('mine')
-    def mine(slot):
+    def mine(slot, with_theirs):
         @each(0, per)
         def _(n):
             cb = slot * per + n
             z = total(MINE, cb)
-            t_copy(swapped(cb)).wait_recv()
+            if with_theirs:
+                t_copy(swapped(cb)).wait_recv()
+                z = z.astype(BF).astype(F32) + zt[swapped(cb)].astype(F32)
             cols = span(me.slots[slot] * per + n, CB)
-            y[:, cols] = (x[:, cols].astype(F32) + (z.astype(BF).astype(F32) + zt[swapped(cb)].astype(F32))).astype(BF)
-
-    @each(0, 3)
-    def _(g):
-        later = (g + 1) // 2
-        lo, n = 2 * (g + later), 2 * (2 - later)
-
-        @pl.when(g == 0)
-        def _():
-            loads[4].wait()
-            loads[5].wait()
-        for k in range(2):
-            @pl.when(g == 1 + k)
-            def _(k=k):
-                with scope('w%d' % k):
-                    to_mate[k].wait_recv()
-        stages(lo, n)
-        if nxt:
+            y[:, cols] = (x[:, cols].astype(F32) + z).astype(BF)
+
+    def wait_rest():
+        loads[4].wait()
+        loads[5].wait()
+
+    if nxt:
+        @each(0, 4)
+        def _(g):
+            n = 2 * per // (1 + g)
+            lo = nb - 2 * n + g // 3
+            pl.when(g == 0)(wait_rest)
+            for k in range(len(to_mate)):
+                @pl.when(g == 1 + k)
+                def _(k=k):
+                    with scope('w%d' % k):
+                        to_mate[k].wait_recv()
+            depart(lo, n)
+
             @pl.when(g == 0)
             def _():
+                join(lo, n)
                 with scope('passing'):
                     for t, f in zip(to_t, on):
                         t.wait_recv()
                         f.start()
-        theirs(lo, lo + n)
+
+            @pl.when(g == 1)
+            def _():
+                theirs(0, 2 * per)
+
+            @pl.when(g == 2)
+            def _():
+                join(2 * per, per)
+                theirs(2 * per, 3 * per)
+        join(3 * per, per)
+        theirs(3 * per, nb)
+    else:
+        @each(0, 2)
+        def _(g):
+            give(g, 1 + 2 * g)
+
+            @pl.when(g == 0)
+            def _():
+                wait_rest()
+
+            @pl.when(g == 1)
+            def _():
+                take(per * OWN, per)
+                theirs(per * MATE, per * FAR)
+                with scope('w'):
+                    for c in to_mate:
+                        c.wait_recv()
+            depart(per * (MATE + g), per)
+            join(per * (MATE + g), per)
+        take(per * PART, per)
+        theirs(per * FAR, nb)
     for slot in SLOTS:
-        mine(slot)
+        mine(slot, nxt or slot in (MATE, FAR))
 
     with scope('end'):
         @each(0, nb)
@@ -857,7 +1006,7 @@
     args = [x, om, s_o, t_o, wo, wd]
     if not last:
         args += [wq, wg, wu]
-        for n in (AHEAD, NT, AHEAD):
+        for n in AHEAD:
             outs += [sds((d4, nq), BF), sds((n, d4, 2 * nf // NT), BF)]
         specs += [ANY] * 6
     npiece = 1 + 2 * NT
@@ -868,7 +1017,7 @@
             pltpu.VMEM((2, t, k), BF), pltpu.VMEM((4, k, d4), BF),
             pltpu.VMEM((4, 2, nb, *unit), BF), pltpu.VMEM((2, nb, *unit), BF), pltpu.VMEM((2, 2, nb, *unit), BF), pltpu.VMEM((nb, *unit), BF),
             pltpu.VMEM((RING, *unit), BF), pltpu.VMEM((LAG + 1, 2 * tok, CB), F32),
-            DMA((6,)), DMA((2,)), DMA((2,)), DMA((3, npiece)), DMA((3, npiece)), DMA((RING,)), DMA((4, 2, nb)),
+            DMA((6,)), DMA((3,)), DMA((3,)), DMA((3, npiece)), DMA((3, npiece)), DMA((RING,)), DMA((4, 2, nb)),
             DMA((2, nb)), DMA((2, nb)), DMA((2, 2, nb)), DMA((2, 2, nb)), DMA((nb,)), DMA((nb,))],
         compiler_params=pltpu.CompilerParams(vmem_limit_bytes=VMEM_LIMIT, collective_id=2 * layer + 1, has_side_effects=True),
         cost_estimate=pl.CostEstimate(flops=4 * t * k * d, bytes_accessed=2 * (2 * t * k + 4 * k * d4), transcendentals=0),
@@ -884,9 +1033,9 @@
         x = x[0]
         gam = jnp.zeros((8, gamma.shape[1]), F32).at[:layers].set(gamma.astype(F32))
         lens = jnp.broadcast_to(lengths.astype(F32)[:, None], (8, 128))
-        om, _, s_o, t_o, wkvb, gam, lens = front(0, mesh, x, gam, lens, weights, ())
+        om, _, s_o, t_o, sg1, wkvb, gam, lens = front(0, mesh, x, gam, lens, weights, ())
         x, *ahead = back(0, mesh, x, om, s_o, t_o, weights, False)
-        om, _, s_o, t_o = front(1, mesh, x, gam, lens, weights, (wkvb, *ahead))
+        om, _, s_o, t_o = front(1, mesh, x, gam, lens, weights, (sg1, wkvb, *ahead))
         (x,) = back(1, mesh, x, om, s_o, t_o, weights, True)
         return x[None]
 

time: 810 us -> 775 us (0.957)
  Pallas kernels: 804 us -> 767 us
    pallas_call x2, Pallas kernels: 494 us -> 473 us  [front(): pl.pallas_call(functools.partial(front_kernel, layer, chips), out_shape=o...]
    pallas_call x2, Pallas kernels: 309 us -> 294 us  [back(): pl.pallas_call(functools.partial(back_kernel, layer, mp // 2, not last),...]
where the time goes in v2:
time: 775 us; the launch traced here: 773 us
  Pallas kernels  767 us (99%)
    pallas_call x2, Pallas kernels, front(): pl.pallas_call(functools.partial(front_kernel, layer, chips), out_shape=o...  473 us
    pallas_call x2, Pallas kernels, back(): pl.pallas_call(functools.partial(back_kernel, layer, mp // 2, not last),...  294 us

profile of v2, /device:TPU:97, one launch (start us, length us, event | category | flops | bytes accessed | tf_op | source)
XLA Modules:
  0.0 772.6 jit_solution(9613570207478654783)
XLA Ops:
  0.7 0.6 broadcast_in_dim.13.refs_2_
  1.2 1.3 pad_convert_fusion.refs_1_
  2.5 261.3 %front0.1 = (bf16[2,2048,1280]{2,1,0:T(8,128)(2,1)}, bf16[2,2048,4096]{2,1,0:T(8,128)(2,1)}, bf16[768,1024]{1,0:T(8,128)(2,1)}, bf16[1280,1024]{1,0:T(8,128)(2,1...) custom-call(bf16[256,4096]{1,0:T(8,128)(2,1)} %bitcast.4, ...), custom_call_target="tpu_custom_call" | custom-call | flops 94489280512 | bytes 100663296 | tf_op jit(solution)/shard_map/front0/pallas_call | solution.py:681
  263.9 164.9 %back0.1 = (bf16[256,4096]{1,0:T(8,128)(2,1)}, bf16[1024,256]{1,0:T(8,128)(2,1)}, bf16[1,1024,512]{2,1,0:T(8,128)(2,1)}, bf16[1024,256]{1,0:T(8,128)(2,1)}, bf16...) custom-call(bf16[256,4096]{1,0:T(8,128)(2,1)} %bitcast.5, ...), custom_call_target="tpu_custom_call" | custom-call | flops 42949672960 | bytes 20971520 | tf_op jit(solution)/shard_map/back0/pallas_call | solution.py:1013
  428.8 211.5 %front1.1 = (bf16[2,2048,1280]{2,1,0:T(8,128)(2,1)}, bf16[2,2048,4096]{2,1,0:T(8,128)(2,1)}, bf16[1280,1024]{1,0:T(8,128)(2,1)}, bf16[1280,1024]{1,0:T(8,128)(2,1)}) custom-call(bf16[256,4096]{1,0:T(8,128)(2,1)} %get-tuple-element.37.refs_0_, f32[4,8,1024]{2,1,0:T(8,128)} %get-tuple-element.38.refs_1_, f32[3,8,128]{2,1,0:T(8,128)} %get-tuple-element.39.refs_2_, ...), custom_call_target="tpu_custom_call" | custom-call | flops 94489280512 | bytes 100663296 | tf_op jit(solution)/shard_map/front1/pallas_call | solution.py:681
  640.3 129.2 %back1.1 = bf16[256,4096]{1,0:T(8,128)(2,1)} custom-call(bf16[256,4096]{1,0:T(8,128)(2,1)} %get-tuple-element.37.refs_0_, bf16[2,2048,1280]{2,1,0:T(8,128)(2,1)} %get-tuple-element.48.refs_1_, bf16[1280,1024]{1,0:T(8,128)(2,1)} %get-tuple-element.49.refs_2_, bf16[1280,1024]{1,0:T(8,128)(2,1)} %get-tuple-element.50.refs_3_, bf16[2,512,1024]{2,1,0:T(8,128)(2,1)} %refs_4_.7, ...), custom_call_target="tpu_custom_call" | custom-call | flops 42949672960 | bytes 20971520 | tf_op jit(solution)/shard_map/back1/pallas_call | solution.py:1013
  769.5 3.1 copy.12

commit v3 on v2

--- a/solution.py
+++ b/solution.py
@@ -580,7 +580,7 @@
         @each(0, 2)
         def _(b):
             with scope('sweep'):
-                sweep(b, True, b, {chips: lambda: gb2.has(SIB), chips + 1: both(near_of(gb2), lambda: relay(2)),
+                sweep(b, True, b, {chips: both(lambda: gb2.has(SIB), gb2.near), chips + 1: both(lambda: gb2.has(SHARE), lambda: relay(2)),
                                    chips + 3: far_of(gb2)}, {})
 
             @pl.when(b == MINE)
@@ -672,7 +672,7 @@
     t = tok * mp
     kvr = wkv.shape[1] // mp
     sds = jax.ShapeDtypeStruct
-    outs = [sds((2, t, nq + nf), BF), sds((2, t, d), BF), sds((no + (nd // 2 if first else nd), d4), BF), sds((no + nd, d4), BF)]
+    outs = [sds((2, t, nq + nf), BF), sds((2, t, d), BF), sds((no + (nd // 4 if first else nd), d4), BF), sds((no + nd, d4), BF)]
     specs = [ANY] * 4
     if first:
         outs += [sds((d4, 2 * nf // NT), BF), sds((2, mp, 4, kvr, nkv), BF), sds((4, *gam.shape), F32), sds((3, *lens.shape), F32)]

time: 775 us -> 775 us (level)
    pallas_call x2, Pallas kernels: 294 us -> 302 us  [back(): pl.pallas_call(functools.partial(back_kernel, layer, mp // 2, not last),...]
where the time goes in v3:
time: 775 us; the launch traced here: 773 us
  Pallas kernels  768 us (99%)
    pallas_call x2, Pallas kernels, front(): pl.pallas_call(functools.partial(front_kernel, layer, chips), out_shape=o...  465 us
    pallas_call x2, Pallas kernels, back(): pl.pallas_call(functools.partial(back_kernel, layer, mp // 2, not last),...  302 us

profile of v3, /device:TPU:97, one launch (start us, length us, event | category | flops | bytes accessed | tf_op | source)
XLA Modules:
  0.0 773.4 jit_solution(9883997456034931239)
XLA Ops:
  0.7 0.6 broadcast_in_dim.13.refs_2_
  1.2 1.3 pad_convert_fusion.refs_1_
  2.5 254.0 %front0.1 = (bf16[2,2048,1280]{2,1,0:T(8,128)(2,1)}, bf16[2,2048,4096]{2,1,0:T(8,128)(2,1)}, bf16[512,1024]{1,0:T(8,128)(2,1)}, bf16[1280,1024]{1,0:T(8,128)(2,1...) custom-call(bf16[256,4096]{1,0:T(8,128)(2,1)} %bitcast.4, ...), custom_call_target="tpu_custom_call" | custom-call | flops 94489280512 | bytes 100663296 | tf_op jit(solution)/shard_map/front0/pallas_call | solution.py:681
  256.5 172.1 %back0.1 = (bf16[256,4096]{1,0:T(8,128)(2,1)}, bf16[1024,256]{1,0:T(8,128)(2,1)}, bf16[1,1024,512]{2,1,0:T(8,128)(2,1)}, bf16[1024,256]{1,0:T(8,128)(2,1)}, bf16...) custom-call(bf16[256,4096]{1,0:T(8,128)(2,1)} %bitcast.5, ...), custom_call_target="tpu_custom_call" | custom-call | flops 42949672960 | bytes 20971520 | tf_op jit(solution)/shard_map/back0/pallas_call | solution.py:1013
  428.7 211.5 %front1.1 = (bf16[2,2048,1280]{2,1,0:T(8,128)(2,1)}, bf16[2,2048,4096]{2,1,0:T(8,128)(2,1)}, bf16[1280,1024]{1,0:T(8,128)(2,1)}, bf16[1280,1024]{1,0:T(8,128)(2,1)}) custom-call(bf16[256,4096]{1,0:T(8,128)(2,1)} %get-tuple-element.37.refs_0_, f32[4,8,1024]{2,1,0:T(8,128)} %get-tuple-element.38.refs_1_, f32[3,8,128]{2,1,0:T(8,128)} %get-tuple-element.39.refs_2_, ...), custom_call_target="tpu_custom_call" | custom-call | flops 94489280512 | bytes 100663296 | tf_op jit(solution)/shard_map/front1/pallas_call | solution.py:681
  640.2 130.0 %back1.1 = bf16[256,4096]{1,0:T(8,128)(2,1)} custom-call(bf16[256,4096]{1,0:T(8,128)(2,1)} %get-tuple-element.37.refs_0_, bf16[2,2048,1280]{2,1,0:T(8,128)(2,1)} %get-tuple-element.48.refs_1_, bf16[1280,1024]{1,0:T(8,128)(2,1)} %get-tuple-element.49.refs_2_, bf16[1280,1024]{1,0:T(8,128)(2,1)} %get-tuple-element.50.refs_3_, bf16[2,512,1024]{2,1,0:T(8,128)(2,1)} %refs_4_.7, ...), custom_call_target="tpu_custom_call" | custom-call | flops 42949672960 | bytes 20971520 | tf_op jit(solution)/shard_map/back1/pallas_call | solution.py:1013
  770.2 3.1 copy.12
